TPU v7x, 32 devices: a whole 2x2x4 slice. The times are simulated.
32 devices in a mesh: gx: 4 (over z), gy: 4 (over x, core), gz: 2 (over y).
Axes of the slice: x: 2, y: 2, z: 4, core: 2. Of those that a mesh axis runs over, the one named last changes fastest.
Arguments:
- residual: float32 [32, 32, 256], P('gx', 'gy', 'gz'), may hold values from -18 to 18
- direction: float32 [32, 32, 256], P('gx', 'gy', 'gz'), may hold values from -18 to 18
Outputs:
- powers: float32 [2, 4, 32, 32, 256], P(None, None, 'gx', 'gy', 'gz')
- gram_matrix: float32 [9, 9], replicated
- projections: float32 [9], replicated
All inputs are finite; a program needn't handle non-finite values.
Results may differ from a plain program's by a relative error of at most 0.00029.
Values sent between devices are 32-bit elements; how exact they have to be, the bound alone decides.
A program may use at most 64 MiB of HBM per device.

v0:
```python
import functools

import jax
import jax.numpy as jnp
from jax import lax
from jax.experimental import pallas as pl
from jax.experimental.pallas import tpu as pltpu
from jax.sharding import PartitionSpec as P

STEPS = 4
SWEEPS = 3
LANES = 128
MESH = pl.DeviceIdType.MESH
HIGHEST = lax.Precision.HIGHEST


def shift_lanes(values, amount):
    amount = amount % LANES
    return values if amount == 0 else pltpu.roll(values, amount, 1)


def kernel(
    counts, dims, res_ref, dir_ref, pow_ref, gram_ref, proj_ref,
    v_ref, t_ref, ysend, yrecv, zsend, zrecv, xsend, xrecv,
    red0, red1,
    ys_sem, yr_sem, zs_sem, zr_sem, xs_sem, xr_sem,
    s0_sem, r0_sem, s1_sem, r1_sem,
):
    nx, ny, nz = counts
    cx, cy, cz = dims
    pitch = cy + 4
    rows = cz + 16
    gx, gy, gz = lax.axis_index("gx"), lax.axis_index("gy"), lax.axis_index("gz")
    here = {"gx": gx, "gy": gy, "gz": gz}
    size = {"gx": nx, "gy": ny, "gz": nz}

    def exists(offset):
        ok = None
        for axis, step in offset.items():
            if step == 0:
                continue
            test = here[axis] + step >= 0 if step < 0 else here[axis] + step < size[axis]
            ok = test if ok is None else jnp.logical_and(ok, test)
        return ok

    def target(offset):
        return {axis: here[axis] + step for axis, step in offset.items() if step != 0}

    yz_offsets = [{"gy": dy, "gz": dz} for dy in (-1, 0, 1) for dz in (-1, 1)]
    y_offsets = [{"gy": -1}, {"gy": 1}]
    x_offsets = [{"gx": -1}, {"gx": 1}]

    barrier = pltpu.get_barrier_semaphore()
    expected = (nx - 1) + (ny * nz - 1)

    def in_line(k):
        return {"gx": lax.rem(gx + k, nx)}

    def in_plane(k):
        ky, kz = divmod(k, nz)
        place = {}
        if ky:
            place["gy"] = lax.rem(gy + ky, ny)
        if kz:
            place["gz"] = lax.rem(gz + kz, nz)
        return place

    for count, place in ((nx, in_line), (ny * nz, in_plane)):
        for k in range(1, count):
            pl.semaphore_signal(barrier, inc=1, device_id=place(k), device_id_type=MESH)

    lane = lax.broadcasted_iota(jnp.int32, (rows, LANES), 1)
    row = lax.broadcasted_iota(jnp.int32, (rows, LANES), 0)
    slot_x = lane // pitch
    slot_y = lane - slot_x * pitch
    at_x, at_y, at_z = slot_x - 1, slot_y - 2, row - 8
    own = (at_x >= 0) & (at_x < cx) & (at_y >= 0) & (at_y < cy) & (at_z >= 0) & (at_z < cz)
    sub = (
        (at_x >= -1) & (at_x <= cx) & (at_y >= -1) & (at_y <= cy) & (at_z >= -1) & (at_z <= cz)
        & (gx * cx + at_x >= 0) & (gx * cx + at_x < nx * cx)
        & (gy * cy + at_y >= 0) & (gy * cy + at_y < ny * cy)
        & (gz * cz + at_z >= 0) & (gz * cz + at_z < nz * cz)
    )

    pick_cell = lax.broadcasted_iota(jnp.int32, (cx * cy, LANES), 0)
    pick_lane = lax.broadcasted_iota(jnp.int32, (cx * cy, LANES), 1)
    pick = (pick_lane == (pick_cell // cy + 1) * pitch + pick_cell % cy + 2).astype(jnp.float32)

    def spread(block_ref):
        flat = block_ref[...].reshape(cx * cy, cz)
        return lax.dot_general(
            flat, pick, (((0,), (0,)), ((), ())), precision=HIGHEST,
            preferred_element_type=jnp.float32,
        )

    def collect(field):
        flat = lax.dot_general(
            pick, field, (((1,), (1,)), ((), ())), precision=HIGHEST,
            preferred_element_type=jnp.float32,
        )
        return flat.reshape(cx, cy, cz)

    def neighbours(u):
        return (
            jnp.where(lane >= pitch, shift_lanes(u, pitch), 0.0)
            + jnp.where(lane < cx * pitch + pitch, shift_lanes(u, -pitch), 0.0) + shift_lanes(u, 1) + shift_lanes(u, -1)
            + pltpu.roll(u, 1, 0) + pltpu.roll(u, rows - 1, 0)
        )

    edge = jnp.zeros((8, LANES), jnp.float32)
    residual_rows = spread(res_ref)
    u0 = jnp.concatenate([edge, spread(dir_ref), edge], axis=0)
    u1 = jnp.concatenate([edge, residual_rows, edge], axis=0)
    v_ref[2 * STEPS + 1] = residual_rows
    t_ref[...] = jnp.zeros_like(t_ref)
    for index, offset in enumerate(y_offsets):
        @pl.when(jnp.logical_not(exists({"gy": -offset["gy"]})))
        def _():
            for r in range(STEPS + 1):
                yrecv[r, index] = jnp.zeros((rows, LANES), jnp.float32)
    for index, offset in enumerate(x_offsets):
        @pl.when(jnp.logical_not(exists({"gx": -offset["gx"]})))
        def _():
            for r in range(STEPS + 1):
                xrecv[r, index] = jnp.zeros((rows, LANES), jnp.float32)
    for index, offset in enumerate(yz_offsets):
        @pl.when(jnp.logical_not(exists({k: -s for k, s in offset.items()})))
        def _():
            for r in range(STEPS + 1):
                zrecv[r, index] = jnp.zeros((8, LANES), jnp.float32)

    pl.semaphore_wait(barrier, expected)

    def copy_y(r, index):
        return pltpu.make_async_remote_copy(
            ysend.at[r, index], yrecv.at[r, index], ys_sem.at[r, index], yr_sem.at[r, index],
            device_id=target(y_offsets[index]), device_id_type=MESH)

    def copy_x(r, index):
        return pltpu.make_async_remote_copy(
            xsend.at[r, index], xrecv.at[r, index], xs_sem.at[r, index], xr_sem.at[r, index],
            device_id=target(x_offsets[index]), device_id_type=MESH)

    def copy_z(r, index):
        side = 0 if yz_offsets[index]["gz"] < 0 else 1
        return pltpu.make_async_remote_copy(
            zsend.at[r, side], zrecv.at[r, index], zs_sem.at[r, index], zr_sem.at[r, index],
            device_id=target(yz_offsets[index]), device_id_type=MESH)

    def start(make, r, offsets):
        for index, offset in enumerate(offsets):
            @pl.when(exists(offset))
            def _():
                make(r, index).start()

    def wait(make, r, offsets):
        for index, offset in enumerate(offsets):
            @pl.when(exists({k: -s for k, s in offset.items()}))
            def _():
                make(r, index).wait_recv()

    def wait_sent(make, r, offsets):
        for index, offset in enumerate(offsets):
            @pl.when(exists(offset))
            def _():
                make(r, index).wait_send()

    def dot_rows(a, b):
        return jnp.sum(a * b, axis=0, keepdims=True)

    total = 2 * STEPS + 1
    pending = None

    def account(r, images):
        fresh = [r] + ([STEPS + r] if r > 0 else [])
        done = list(range(r + 1)) + [STEPS + 1 + k for k in range(r)]
        for a in fresh:
            image = images[0] if a == r else images[1]
            for b in done:
                if a == r and b == STEPS + r and r > 0:
                    continue
                part = dot_rows(v_ref[b], image)
                t_ref[pl.ds(a * total + b, 1), :] = part
                if a != b:
                    t_ref[pl.ds(b * total + a, 1), :] = part
            t_ref[pl.ds(total * total + a, 1), :] = dot_rows(v_ref[a], v_ref[total])

    def emit(r):
        if r > 0:
            pow_ref[0, r - 1] = collect(v_ref[r])
            pow_ref[1, r - 1] = collect(v_ref[STEPS + r])

    low = lambda v: jnp.where(slot_y < 3, v, 0.0)
    span = lambda start_lane, stop_lane: (lane >= start_lane) & (lane < stop_lane)
    top = cx * pitch
    for r in range(STEPS + 1):
        for side, head in ((0, 7), (1, cz + 6)):
            zsend[r, side] = jnp.concatenate(
                [u0[head:head + 3], u1[head:head + 3], jnp.zeros((2, LANES), jnp.float32)], axis=0)
        ysend[r, 0] = jnp.where(slot_y >= 9, shift_lanes(u0, cy), shift_lanes(u1, cy - 3))
        ysend[r, 1] = jnp.where(slot_y < 3, shift_lanes(u0, -cy), shift_lanes(u1, 3 - cy))
        start(copy_z, r, yz_offsets)
        start(copy_y, r, y_offsets)
        if pending is not None:
            account(r - 1, pending)
        wait(copy_y, r, y_offsets)
        from_above, from_below = yrecv[r, 0], yrecv[r, 1]
        p0 = u0 + jnp.where(slot_y >= 9, from_above, 0.0) + low(from_below)
        p1 = (
            u1 + jnp.where(slot_y >= 9, shift_lanes(from_above, 3), 0.0)
            + low(shift_lanes(from_below, -3))
        )
        wait(copy_z, r, yz_offsets)
        tile_slot = slot_y[:8]
        tiles = []
        for side in (0, 1):
            mid = zrecv[r, 2 + side]
            down = jnp.where(tile_slot >= 9, shift_lanes(zrecv[r, side], cy), 0.0)
            up = jnp.where(tile_slot < 3, shift_lanes(zrecv[r, 4 + side], -cy), 0.0)
            tiles.append(mid + down + up)

        def with_tiles(p, first):
            upper, lower = tiles[0][first:first + 3], tiles[1][first:first + 3]
            zero = lambda n: jnp.zeros((n, LANES), jnp.float32)
            head = p[:16] + jnp.concatenate([zero(6), lower, zero(7)], axis=0)
            tail = p[rows - 16:] + jnp.concatenate([zero(7), upper, zero(6)], axis=0)
            return jnp.concatenate([head, p[16:rows - 16], tail], axis=0)

        p0, p1 = with_tiles(p0, 0), with_tiles(p1, 3)
        width = 3 * pitch
        xsend[r, 0] = jnp.where(lane < width, p0, shift_lanes(p1, width))
        far = (cx - 1) * pitch
        xsend[r, 1] = jnp.where(lane < width, shift_lanes(p0, -far), shift_lanes(p1, width - far))
        start(copy_x, r, x_offsets)
        if r > 0:
            emit(r - 1)
        wait(copy_x, r, x_offsets)
        beyond, before = xrecv[r, 0], xrecv[r, 1]
        at_low, at_high = span(0, 2 * pitch), span(top, top + 2 * pitch)
        ext_low, ext_high = span(0, pitch), span(top + pitch, top + 2 * pitch)

        def with_x(p, first):
            main = (
                p + jnp.where(at_low, shift_lanes(before, -first - pitch), 0.0)
                + jnp.where(at_high, shift_lanes(beyond, top - first), 0.0)
            )
            far_cells = (
                jnp.where(ext_low, shift_lanes(before, -first), 0.0)
                + jnp.where(ext_high, shift_lanes(beyond, top - pitch - first), 0.0)
            )
            return main, far_cells

        p0, far0 = with_x(p0, 0)
        p1, far1 = with_x(p1, width)
        p0 = jnp.where(lane < top + 2 * pitch, p0, 0.0)
        p1 = jnp.where(lane < top + 2 * pitch, p1, 0.0)
        b0 = jnp.where(sub, 6.0 * p0 - neighbours(p0) - far0, 0.0)
        a1 = jnp.where(sub, 6.0 * p1 - neighbours(p1) - far1, 0.0)
        b1 = jnp.where(sub, p1, 0.0) if r == 0 else a1
        v_ref[r] = jnp.where(own, p0, 0.0)[8:8 + cz]
        if r > 0:
            v_ref[STEPS + r] = jnp.where(own, p1, 0.0)[8:8 + cz]
        pending = (b0[8:8 + cz], a1[8:8 + cz])
        if r < STEPS:
            c0, c1 = b0 * (1.0 / 9.0), b1 * (1.0 / 9.0)
            u0, u1 = c0, c1
            for _ in range(SWEEPS - 1):
                u0 = jnp.where(sub, c0 + u0 * (1.0 / 3.0) + neighbours(u0) * (1.0 / 9.0), 0.0)
                u1 = jnp.where(sub, c1 + u1 * (1.0 / 3.0) + neighbours(u1) * (1.0 / 9.0), 0.0)

    account(STEPS, pending)
    value = lax.dot_general(
        jnp.ones((8, LANES), jnp.float32), t_ref[...], (((1,), (1,)), ((), ())),
        precision=HIGHEST, preferred_element_type=jnp.float32)

    def gather(value, count, place, slots, buffer, s_sem, r_sem, first):
        buffer[0] = value

        def make(k):
            return pltpu.make_async_remote_copy(
                buffer.at[0], buffer.at[k], s_sem.at[k], r_sem.at[k],
                device_id=place(k), device_id_type=MESH)

        for k in range(1, count):
            make(k).start()
        if first:
            emit(STEPS)
        for k in range(1, count):
            make(k).wait_recv()
        result = jnp.zeros_like(value)
        for slot in slots:
            result = result + buffer[slot]
        for k in range(1, count):
            make(k).wait_send()
        return result

    plane_slots = [
        lax.rem(gy + ny - g, ny) * nz + lax.rem(gz + nz - h, nz)
        for g in range(ny) for h in range(nz)
    ]
    line_slots = [lax.rem(gx + nx - g, nx) for g in range(nx)]
    value = gather(value, ny * nz, in_plane, plane_slots, red0, s0_sem, r0_sem, True)
    value = gather(value, nx, in_line, line_slots, red1, s1_sem, r1_sem, False)
    value = value * (1.0 / (nx * cx * ny * cy * nz * cz))
    for a in range(total):
        gram_ref[a:a + 1, :] = value[0:1, a * total:(a + 1) * total]
    proj_ref[...] = value[0:1, total * total:total * total + total]
    for r in range(STEPS + 1):
        wait_sent(copy_y, r, y_offsets)
        wait_sent(copy_z, r, yz_offsets)
        wait_sent(copy_x, r, x_offsets)


def solution(mesh):
    counts = tuple(mesh.shape[a] for a in ("gx", "gy", "gz"))

    def local(residual, direction):
        dims = residual.shape
        rows = dims[2] + 16
        total = 2 * STEPS + 1
        rounds = STEPS + 1
        f32 = jnp.float32
        dma = pltpu.SemaphoreType.DMA
        vm = pl.BlockSpec(memory_space=pltpu.VMEM)
        powers, gram, proj = pl.pallas_call(
            functools.partial(kernel, counts, dims),
            out_shape=(
                jax.ShapeDtypeStruct((2, STEPS) + dims, f32),
                jax.ShapeDtypeStruct((total, total), f32),
                jax.ShapeDtypeStruct((1, total), f32),
            ),
            in_specs=[vm, vm],
            out_specs=(vm, vm, vm),
            scratch_shapes=[
                pltpu.VMEM((total + 1, dims[2], LANES), f32),
                pltpu.VMEM((LANES, LANES), f32),
                pltpu.VMEM((rounds, 2, rows, LANES), f32),
                pltpu.VMEM((rounds, 2, rows, LANES), f32),
                pltpu.VMEM((rounds, 2, 8, LANES), f32),
                pltpu.VMEM((rounds, 6, 8, LANES), f32),
                pltpu.VMEM((rounds, 2, rows, LANES), f32),
                pltpu.VMEM((rounds, 2, rows, LANES), f32),
                pltpu.VMEM((counts[1] * counts[2], 8, LANES), f32),
                pltpu.VMEM((counts[0], 8, LANES), f32),
                dma((rounds, 2)), dma((rounds, 2)),
                dma((rounds, 6)), dma((rounds, 6)),
                dma((rounds, 2)), dma((rounds, 2)),
                dma((counts[1] * counts[2],)), dma((counts[1] * counts[2],)),
                dma((counts[0],)), dma((counts[0],)),
            ],
            compiler_params=pltpu.CompilerParams(collective_id=0, has_side_effects=True),
            name="powers_basis",
        )(residual, direction)
        return powers, gram, proj.reshape(total)

    placed = (P("gx", "gy", "gz"), P("gx", "gy", "gz"))
    return jax.shard_map(
        local,
        mesh=mesh,
        in_specs=placed,
        out_specs=(P(None, None, "gx", "gy", "gz"), P(), P()),
        check_vma=False,
    )
```

profile of v0, /device:TPU:0, one launch (start us, length us, event | category | flops | bytes accessed | tf_op | source)
XLA Modules:
  0.0 55.4 jit_solution(1383204819106254284)
XLA Ops:
  0.6 51.9 %powers_basis.1 = (f32[2,4,8,8,128]{4,3,2,1,0:T(8,128)}, f32[9,9]{1,0:T(8,128)}, f32[1,9]{1,0:T(1,128)}) custom-call(f32[8,8,128]{2,1,0:T(8,128)} %res_ref.1, f32[8,8,128]{2,1,0:T(8,128)} %dir_ref.1), custom_call_target="tpu_custom_call" | custom-call | tf_op jit(solution)/shard_map/powers_basis/pallas_call | solution.py:325
  52.5 0.0 copy-start
  52.5 1.7 %copy.8 = f32[2,4,8,8,128]{4,3,2,1,0:T(8,128)} copy(f32[2,4,8,8,128]{4,3,2,1,0:T(8,128)} %get-tuple-element.12) | data formatting | bytes 524288
  54.2 0.0 copy-done
  54.2 0.0 copy-start.1
  54.2 0.6 %copy.9 = f32[9,9]{1,0:T(8,128)} copy(f32[9,9]{1,0:T(8,128)S(1)} %copy-done) | data formatting | bytes 648
  54.8 0.1 copy-done.1
  54.9 0.5 copy.10
Async XLA Ops:
  52.5 1.7 %copy-start = (f32[9,9]{1,0:T(8,128)S(1)}, f32[9,9]{1,0:T(8,128)}, u32[]{:S(2)}) copy-start(f32[9,9]{1,0:T(8,128)} %get-tuple-element.13) | copy-start | bytes 976
  54.2 0.7 %copy-start.1 = (f32[1,9]{1,0:T(1,128)S(1)}, f32[1,9]{1,0:T(1,128)}, u32[]{:S(2)}) copy-start(f32[1,9]{1,0:T(1,128)} %get-tuple-element.8) | copy-start | bytes 112
where the time goes:
time: 55.6 us; the launch traced here: 55.4 us
  Pallas kernels  51.9 us (93%)
  local copies, waits for them, and re-layouts  2.87 us (5%)
  between operations  0.65 us (1%)
    pallas_call x1, Pallas kernels, local(): pl.pallas_call(functools.partial(kernel, counts, dims), out_shape=(jax.Sh...  51.9 us
    unnamed x7, local copies, waits for them, and re-layouts  2.87 us

commit v1 on v0

v1 whole, which is shorter than its diff:
```python
import functools

import jax
import jax.numpy as jnp
from jax import lax
from jax.experimental import pallas as pl
from jax.experimental.pallas import tpu as pltpu
from jax.sharding import PartitionSpec as P

STEPS = 4
LANES = 128
MESH = pl.DeviceIdType.MESH
HIGHEST = lax.Precision.HIGHEST
F32 = jnp.float32
AXES = ("gx", "gy", "gz")
GAMMA, BETA, ALPHA, DELTA = 13.0 / 81.0, 5.0 / 243.0, 1.0 / 729.0, 1.0 / 1458.0
P_CHAIN, Z_CHAIN = 0, 1
REACH = ((6, 5), (7, 7))
CHUNK = 4
OFFSETS = [(dx, dy, dz) for dx in (-1, 0, 1) for dy in (-1, 0, 1) for dz in (-1, 0, 1) if (dx, dy, dz) != (0, 0, 0)]


def as_f32(flag):
    return jnp.where(flag, 1.0, 0.0).astype(F32)


def axis_terms(at, width, low, high, place, count):
    inside = (place * width + at >= 0) & (place * width + at < count * width)
    cover = ((at == -1) | (at == 0)) & low | ((at == width - 1) | (at == width)) & high
    inner = ((at == -2) | (at == 1)) & low | ((at == width - 2) | (at == width + 1)) & high
    below = (at == 1) & low | (at == width + 1) & high
    above = (at == -2) & low | (at == width - 2) & high
    mask = as_f32(inside)
    return (1.0 + as_f32(cover)) * mask, as_f32(inner), 1.0 - 0.5 * as_f32(below), 1.0 - 0.5 * as_f32(above), mask


def kernel(
    counts, dims, near, res_ref, dir_ref, pow_ref, gram_ref, proj_ref,
    main, pack, got, face, cbuf, czbuf, sbuf, szbuf, image, base, tab, ztab, t_ref, red0, red1,
    in_sem, out_sem, s_sem, r_sem, s0_sem, r0_sem, s1_sem, r1_sem,
):
    nx, ny, nz = counts
    cx, cy, cz = dims
    group = LANES // cx
    half = group // 2
    rows = 3 * cy
    place = [lax.axis_index(a) for a in AXES]
    gx, gy, gz = place
    low = [place[i] > 0 for i in range(3)]
    high = [place[i] < counts[i] - 1 for i in range(3)]
    total = 2 * STEPS + 1

    def exists(offset):
        ok = None
        for i, step in enumerate(offset):
            if step:
                test = low[i] if step < 0 else high[i]
                ok = test if ok is None else jnp.logical_and(ok, test)
        return ok

    def flip(offset):
        return tuple(-s for s in offset)

    def target(offset):
        return {AXES[i]: place[i] + s for i, s in enumerate(offset) if s}

    def ahead(axes):
        def make(k):
            out = {}
            for a in reversed(axes):
                k, step = divmod(k, counts[AXES.index(a)])
                if step:
                    out[a] = lax.rem(place[AXES.index(a)] + step, counts[AXES.index(a)])
            return out
        size = 1
        for a in axes:
            size *= counts[AXES.index(a)]
        return size, make

    loads = [
        pltpu.make_async_copy(ref, main.at[c, 0, pl.ds(cx, cx), pl.ds(cy, cy)], in_sem.at[c])
        for c, ref in ((Z_CHAIN, res_ref), (P_CHAIN, dir_ref))
    ]
    for copy in loads:
        copy.start()

    barrier = pltpu.get_barrier_semaphore()
    expected = 0
    for offset in OFFSETS:
        @pl.when(exists(offset))
        def _():
            pl.semaphore_signal(barrier, 1, device_id=target(offset), device_id_type=MESH)
        expected = expected + exists(offset).astype(jnp.int32)
    if not near:
        for axes in (("gy", "gz"), ("gx",)):
            size, make = ahead(axes)
            for k in range(1, size):
                pl.semaphore_signal(barrier, 1, device_id=make(k), device_id_type=MESH)
            expected = expected + (size - 1)

    fields = [(c, f) for c in (0, 1) for f in (0, 2)]
    for flag, xs, ys in (
        (low[0], pl.ds(0, cx), pl.ds(0, rows)), (high[0], pl.ds(2 * cx, cx), pl.ds(0, rows)),
        (low[1], pl.ds(0, 3 * cx), pl.ds(0, cy)), (high[1], pl.ds(0, 3 * cx), pl.ds(2 * cy, cy)),
    ):
        @pl.when(jnp.logical_not(flag))
        def _():
            for c, f in fields:
                main[c, f, xs, ys] = jnp.zeros((xs.size, ys.size, LANES), F32)
    for flag, ss, xs, ys in (
        (low[2], 0, pl.ds(0, 3), pl.ds(0, rows)), (high[2], 1, pl.ds(0, 3), pl.ds(0, rows)),
        (low[0], None, pl.ds(0, 1), pl.ds(0, rows)), (high[0], None, pl.ds(2, 1), pl.ds(0, rows)),
        (low[1], None, pl.ds(0, 3), pl.ds(0, cy)), (high[1], None, pl.ds(0, 3), pl.ds(2 * cy, cy)),
    ):
        @pl.when(jnp.logical_not(flag))
        def _():
            for c in (0, 1):
                for s in (0, 1):
                    for side in ((0, 1) if ss is None else (ss,)):
                        got[c, s, side, xs, ys] = jnp.zeros((xs.size, ys.size, LANES), F32)

    lane = lax.broadcasted_iota(jnp.int32, (rows, LANES), 1)
    row = lax.broadcasted_iota(jnp.int32, (rows, LANES), 0)
    wy, fy, up_y, down_y, my = axis_terms(row - cy, cy, low[1], high[1], gy, ny)
    wz, fz, up_z, down_z, mz = axis_terms(lane, cz, low[2], high[2], gz, nz)

    def x_terms(x):
        return axis_terms(jnp.int32(x), cx, low[0], high[0], gx, nx)

    D_REPS = (-3, -1, 0, 3, cx - 1, cx, cx + 2)
    D0, AM0, M0, G0, UPY, DOWNY, UPZ, DOWNZ = 0, 7, 10, 13, 18, 19, 20, 21
    wyz, myz, fyz = wy * wz, my * mz, fy + fz
    for k, x in enumerate(D_REPS):
        tab[D0 + k] = wyz * x_terms(x)[0]
    for k, x in enumerate((-3, 3, cx + 2)):
        mask = myz * x_terms(x)[4]
        tab[AM0 + k] = mask * ALPHA
        tab[M0 + k] = mask
    for k, x in enumerate((3, -2, 1, cx - 2, cx + 1)):
        tab[G0 + k] = GAMMA + DELTA * (fyz + x_terms(x)[1])
    tab[UPY], tab[DOWNY], tab[UPZ], tab[DOWNZ] = up_y, down_y, up_z, down_z
    below_1, above_6 = x_terms(1)[2], x_terms(cx - 2)[3]

    slot = (lane + half) // group % cx
    deep = (lane + half) % group - half
    is_hi = deep >= 0
    z_at = jnp.where(is_hi, deep + cz, deep)
    wzz, fzz, up_zz, down_zz, mzz = axis_terms(z_at, cz, low[2], high[2], gz, nz)
    ZD, ZAM, ZM, ZG, ZUX, ZDX, ZUZ, ZDZ = 0, 3, 6, 9, 12, 15, 18, 19
    for b in range(3):
        wx, fx, up_x, down_x, mx = axis_terms(slot + (b - 1) * cx, cx, low[0], high[0], gx, nx)
        ztab[ZD + b] = wx * wy * wzz
        ztab[ZAM + b] = mx * my * mzz * ALPHA
        ztab[ZM + b] = mx * my * mzz
        ztab[ZG + b] = GAMMA + DELTA * (fx + fy + fzz)
        ztab[ZUX + b] = up_x
        ztab[ZDX + b] = down_x
    ztab[ZUZ], ztab[ZDZ] = up_zz, down_zz
    first_lane, last_lane = lane == 0, lane == LANES - 1
    at_first, at_last = deep == 0, deep == -1
    first_slot, last_slot = slot == 0, slot == cx - 1

    def d_class(x):
        if x < 0:
            return D0 + (1 if x == -1 else 0)
        if x >= cx:
            return D0 + (5 if x == cx else 6)
        return D0 + (2 if x == 0 else 4 if x == cx - 1 else 3)

    def g_class(x):
        return G0 + {-2: 1, 1: 2, cx - 2: 3, cx + 1: 4}.get(x, 0)

    def roll_rows(v, shift):
        return pltpu.roll(v, shift % v.shape[0], 0)

    def roll_lanes(v, shift):
        shift = shift % LANES
        return v if shift == 0 else pltpu.roll(v, shift, 1)

    def rolled(v, shift, axis):
        flat = v.reshape(-1, LANES)
        return (roll_rows if axis == 0 else roll_lanes)(flat, shift).reshape(v.shape)

    def planes(reach):
        xs = list(range(-reach, cx + reach))
        return [xs[i:i + CHUNK] for i in range(0, len(xs), CHUNK)]

    def table(kind, xs):
        ks = [kind(x) for x in xs]
        if len(set(ks)) == 1:
            return tab[ks[0]][None]
        return jnp.stack([tab[k] for k in ks])

    def unpacked(z_src, xs):
        return jnp.stack([roll_lanes(z_src[(x + cx) // cx], -group * (x % cx)) for x in xs])

    def beside(src, z_src, xs, weighted):
        lo = xs[0] + cx
        mid = src[pl.ds(lo, len(xs))]
        if not weighted or not set(xs) & {1, cx - 2, -2, cx + 1}:
            along_x = src[pl.ds(lo - 1, len(xs))] + src[pl.ds(lo + 1, len(xs))]
        else:
            parts = []
            for x in xs:
                a, b = src[x + cx - 1], src[x + cx + 1]
                if x == 1:
                    a = a * below_1
                if x == cx + 1:
                    a = a * 0.5
                if x == cx - 2:
                    b = b * above_6
                if x == -2:
                    b = b * 0.5
                parts.append(a + b)
            along_x = jnp.stack(parts)
        extra = unpacked(z_src, xs)
        up = rolled(jnp.where(last_lane[None], extra, mid), 1, 1)
        down = rolled(jnp.where(first_lane[None], extra, mid), -1, 1)
        left, right = rolled(mid, 1, 0), rolled(mid, -1, 0)
        if weighted:
            up, down = up * tab[UPZ][None], down * tab[DOWNZ][None]
            left, right = left * tab[UPY][None], right * tab[DOWNY][None]
        return mid, (along_x + (left + right)) + (up + down)

    def z_beside(src, z_src, b, reach, weighted):
        mid = z_src[b]
        inject = jnp.zeros((rows, LANES), F32)
        for g in range(cx):
            x = g + (b - 1) * cx
            if -reach <= x < cx + reach:
                inject = jnp.where(slot_edge[g], roll_lanes(src[x + cx], group * g), inject)
        up = roll_lanes(jnp.where(at_last, inject, mid), 1)
        down = roll_lanes(jnp.where(at_first, inject, mid), -1)
        left, right = roll_rows(mid, 1), roll_rows(mid, -1)
        before, after = roll_lanes(mid, group), roll_lanes(mid, -group)
        if b > 0:
            before = jnp.where(first_slot, roll_lanes(z_src[b - 1], group), before)
        if b < 2:
            after = jnp.where(last_slot, roll_lanes(z_src[b + 1], -group), after)
        if weighted:
            up, down = up * ztab[ZUZ], down * ztab[ZDZ]
            left, right = left * tab[UPY], right * tab[DOWNY]
            before, after = before * ztab[ZUX + b], after * ztab[ZDX + b]
        return mid, ((before + after) + (left + right)) + (up + down)

    slot_edge = [(slot == g) & ((deep == 0) | (deep == -1)) for g in range(cx)]

    def apply_a(c, f, reach, index):
        src, z_src = main.at[c, f], pack.at[c, f]
        for xs in planes(reach):
            mid, around = beside(src, z_src, xs, False)
            value = 6.0 * mid - around
            for i, x in enumerate(xs):
                if 0 <= x < cx:
                    image[index, x] = value[i, cy:2 * cy]
            if reach > 0:
                cbuf[c, pl.ds(xs[0] + cx, len(xs))] = value * table(d_class, xs)
        if reach > 0:
            for b in range(3):
                mid, around = z_beside(src, z_src, b, reach, False)
                czbuf[c, b] = (6.0 * mid - around) * ztab[ZD + b]

    def scale_only(c, f, reach):
        for xs in planes(reach):
            ds = pl.ds(xs[0] + cx, len(xs))
            cbuf[c, ds] = main[c, f, ds] * table(d_class, xs)
        for b in range(3):
            czbuf[c, b] = pack[c, f, b] * ztab[ZD + b]

    def apply_m(c, f, reach):
        src, z_src = cbuf.at[c], czbuf.at[c]
        for xs in planes(reach + 1):
            mid, around = beside(src, z_src, xs, True)
            sbuf[c, pl.ds(xs[0] + cx, len(xs))] = BETA * mid + around * table(lambda x: AM0 + (x + cx) // cx, xs)
        for b in range(3):
            mid, around = z_beside(src, z_src, b, reach + 1, True)
            szbuf[c, b] = BETA * mid + around * ztab[ZAM + b]
        s_src, sz_src = sbuf.at[c], szbuf.at[c]
        for xs in planes(reach):
            ds = pl.ds(xs[0] + cx, len(xs))
            _, around = beside(s_src, sz_src, xs, True)
            value = src[ds] * table(g_class, xs)
            if reach > 0:
                main[c, f, ds] = value + around * table(lambda x: M0 + (x + cx) // cx, xs)
            else:
                main[c, f, ds, pl.ds(cy, cy)] = (value + around)[:, cy:2 * cy]
        if reach > 0:
            for b in range(3):
                _, around = z_beside(s_src, sz_src, b, reach, True)
                pack[c, f, b] = z_src[b] * ztab[ZG + b] + around * ztab[ZM + b]

    def copy_to(c, s, index):
        dx, dy, dz = OFFSETS[index]
        f = 2 * s
        if dz == 0:
            n = cx if dx == 0 else REACH[s][c] - (dy != 0)
            first = cx if dx <= 0 else 2 * cx - n
            there = pl.ds(first - cx * dx, n)
            source = main.at[c, f, pl.ds(first, n), pl.ds(cy, cy)]
            sink = main.at[c, f, there, pl.ds(cy - cy * dy, cy)]
        else:
            source = face.at[c, s]
            sink = got.at[c, s, 0 if dz > 0 else 1, 1 - dx, pl.ds(cy - cy * dy, cy)]
        return pltpu.make_async_remote_copy(
            source, sink, s_sem.at[c, s, index], r_sem.at[c, s, index],
            device_id=target(OFFSETS[index]), device_id_type=MESH)

    def pack_face(c, s):
        f = 2 * s
        value = jnp.zeros((cy, LANES), F32)
        for g in range(cx):
            moved = roll_lanes(main[c, f, cx + g, pl.ds(cy, cy)], group * g)
            value = jnp.where(slot[:cy] == g, moved, value)
        face[c, s] = value

    def send(c, s):
        order = sorted(range(len(OFFSETS)), key=lambda i: -sum(abs(v) for v in OFFSETS[i]))
        for index in order:
            @pl.when(exists(OFFSETS[index]))
            def _():
                copy_to(c, s, index).start()

    def receive(c, s):
        for index, offset in enumerate(OFFSETS):
            @pl.when(exists(flip(offset)))
            def _():
                copy_to(c, s, index).wait_recv()
        pack[c, 2 * s] = jnp.where(is_hi[None], got[c, s, 1], got[c, s, 0])

    def done_sending(c, s):
        for index, offset in enumerate(OFFSETS):
            @pl.when(exists(offset))
            def _():
                copy_to(c, s, index).wait_send()

    def own(c, f):
        return main[c, f, pl.ds(cx, cx), pl.ds(cy, cy)].reshape(cx * cy, LANES)

    outs = []

    def emit(c, f, slot_out):
        copy = pltpu.make_async_copy(
            main.at[c, f, pl.ds(cx, cx), pl.ds(cy, cy)], pow_ref.at[c, slot_out], out_sem.at[c, slot_out])
        copy.start()
        outs.append(copy)

    place_of = {a: (P_CHAIN, a) for a in range(STEPS + 1)}
    place_of.update({STEPS + 1 + k: (Z_CHAIN, k + 1) for k in range(STEPS)})
    ready = []

    def account(a):
        ready.append(a)
        picture = image[a].reshape(cx * cy, LANES)
        for b in ready:
            part = jnp.sum(own(*place_of[b]) * picture, axis=0, keepdims=True)
            t_ref[pl.ds(a * total + b, 1), :] = part
            if a != b:
                t_ref[pl.ds(b * total + a, 1), :] = part
        t_ref[pl.ds(total * total + a, 1), :] = jnp.sum(
            own(*place_of[a]) * own(Z_CHAIN, 0), axis=0, keepdims=True)

    t_ref[...] = jnp.zeros_like(t_ref)
    for copy in loads:
        copy.wait()
    for c in (Z_CHAIN, P_CHAIN):
        pack_face(c, 0)
    pl.semaphore_wait(barrier, expected)
    send(Z_CHAIN, 0)
    send(P_CHAIN, 0)

    first_z = STEPS + 1
    receive(Z_CHAIN, 0)
    scale_only(Z_CHAIN, 0, 5)
    apply_m(Z_CHAIN, 1, 3)
    emit(Z_CHAIN, 1, 0)
    apply_a(Z_CHAIN, 1, 2, first_z)
    apply_m(Z_CHAIN, 2, 0)
    pack_face(Z_CHAIN, 1)
    send(Z_CHAIN, 1)
    emit(Z_CHAIN, 2, 1)

    receive(P_CHAIN, 0)
    apply_a(P_CHAIN, 0, 5, 0)
    apply_m(P_CHAIN, 1, 3)
    emit(P_CHAIN, 1, 0)
    apply_a(P_CHAIN, 1, 2, 1)
    apply_m(P_CHAIN, 2, 0)
    pack_face(P_CHAIN, 1)
    send(P_CHAIN, 1)
    emit(P_CHAIN, 2, 1)
    for a in (0, 1, first_z):
        account(a)

    receive(Z_CHAIN, 1)
    apply_a(Z_CHAIN, 2, 6, first_z + 1)
    apply_m(Z_CHAIN, 3, 4)
    emit(Z_CHAIN, 3, 2)
    apply_a(Z_CHAIN, 3, 3, first_z + 2)
    apply_m(Z_CHAIN, 4, 1)
    emit(Z_CHAIN, 4, 3)
    apply_a(Z_CHAIN, 4, 0, first_z + 3)
    for a in (first_z + 1, first_z + 2, first_z + 3):
        account(a)

    receive(P_CHAIN, 1)
    apply_a(P_CHAIN, 2, 6, 2)
    account(2)
    apply_m(P_CHAIN, 3, 4)
    emit(P_CHAIN, 3, 2)
    apply_a(P_CHAIN, 3, 3, 3)
    account(3)
    apply_m(P_CHAIN, 4, 1)
    emit(P_CHAIN, 4, 3)
    apply_a(P_CHAIN, 4, 0, 4)
    account(4)

    value = lax.dot_general(
        jnp.ones((8, LANES), F32), t_ref[...], (((1,), (1,)), ((), ())),
        precision=HIGHEST, preferred_element_type=F32)[0:1]

    def gather(value, axes, buffer, send_sem, recv_sem):
        size, make = ahead(axes)
        buffer[0] = value

        def copy(k):
            return pltpu.make_async_remote_copy(
                buffer.at[0], buffer.at[k], send_sem.at[k], recv_sem.at[k],
                device_id=make(k), device_id_type=MESH)

        for k in range(1, size):
            copy(k).start()
        for k in range(1, size):
            copy(k).wait_recv()
        result = jnp.zeros_like(value)
        for k in range(size):
            rest, at = k, 0
            scale = 1
            for a in reversed(axes):
                n = counts[AXES.index(a)]
                rest, want = divmod(rest, n)
                at = at + scale * lax.rem(place[AXES.index(a)] + n - want, n)
                scale *= n
            result = result + buffer[at]
        for k in range(1, size):
            copy(k).wait_send()
        return result

    if near:
        value = gather(value, AXES, red0, s0_sem, r0_sem)
    else:
        value = gather(value, ("gy", "gz"), red0, s0_sem, r0_sem)
        value = gather(value, ("gx",), red1, s1_sem, r1_sem)
    value = value * (1.0 / (nx * cx * ny * cy * nz * cz))
    for a in range(total):
        gram_ref[a:a + 1, :] = value[0:1, a * total:(a + 1) * total]
    proj_ref[...] = value[0:1, total * total:total * total + total]
    for c in (0, 1):
        for s in (0, 1):
            done_sending(c, s)
    for copy in outs:
        copy.wait()


def solution(mesh):
    counts = tuple(mesh.shape[a] for a in AXES)
    near = max(counts) <= 4
    devices = counts[0] * counts[1] * counts[2]
    plane = devices if near else counts[1] * counts[2]

    def local(residual, direction):
        dims = residual.shape
        cx, cy, cz = dims
        assert cz == LANES and LANES % cx == 0 and cy % 8 == 0
        assert min(cx, cy, LANES // cx // 2) > max(max(r) for r in REACH)
        total = 2 * STEPS + 1
        fields = STEPS + 1
        dma = pltpu.SemaphoreType.DMA
        vm = pl.BlockSpec(memory_space=pltpu.VMEM)
        hbm = pl.BlockSpec(memory_space=pl.ANY)
        ext = (3 * cx, 3 * cy, LANES)
        zext = (3, 3 * cy, LANES)
        n = len(OFFSETS)
        powers, gram, proj = pl.pallas_call(
            functools.partial(kernel, counts, dims, near),
            out_shape=(
                jax.ShapeDtypeStruct((2, STEPS) + dims, F32),
                jax.ShapeDtypeStruct((total, total), F32),
                jax.ShapeDtypeStruct((1, total), F32),
            ),
            in_specs=[hbm, hbm],
            out_specs=(hbm, vm, vm),
            scratch_shapes=[
                pltpu.VMEM((2, fields) + ext, F32),
                pltpu.VMEM((2, fields) + zext, F32),
                pltpu.VMEM((2, 2, 2) + zext, F32),
                pltpu.VMEM((2, 2, cy, LANES), F32),
                pltpu.VMEM((2,) + ext, F32),
                pltpu.VMEM((2,) + zext, F32),
                pltpu.VMEM((2,) + ext, F32),
                pltpu.VMEM((2,) + zext, F32),
                pltpu.VMEM((total, cx, cy, LANES), F32),
                pltpu.VMEM((1, 8, LANES), F32),
                pltpu.VMEM((22, 3 * cy, LANES), F32),
                pltpu.VMEM((20, 3 * cy, LANES), F32),
                pltpu.VMEM((LANES, LANES), F32),
                pltpu.VMEM((plane, 1, LANES), F32),
                pltpu.VMEM((counts[0], 1, LANES), F32),
                dma((2,)), dma((2, STEPS)),
                dma((2, 2, n)), dma((2, 2, n)),
                dma((plane,)), dma((plane,)),
                dma((counts[0],)), dma((counts[0],)),
            ],
            compiler_params=pltpu.CompilerParams(collective_id=0, has_side_effects=True),
            name="powers_basis",
        )(residual, direction)
        return powers, gram, proj.reshape(total)

    placed = (P("gx", "gy", "gz"), P("gx", "gy", "gz"))
    return jax.shard_map(
        local,
        mesh=mesh,
        in_specs=placed,
        out_specs=(P(None, None, "gx", "gy", "gz"), P(), P()),
        check_vma=False,
    )
```

time: 55.6 us -> 33.1 us (0.60)
  Pallas kernels: 51.9 us -> 29.3 us
    pallas_call x1, Pallas kernels: 51.9 us -> 29.3 us  [local(): pl.pallas_call(functools.partial(kernel, counts, dims, near), out_shape=(...]
where the time goes in v1:
time: 33.1 us; the launch traced here: 32.8 us
  Pallas kernels  29.3 us (89%)
  local copies, waits for them, and re-layouts  2.87 us (9%)
  between operations  0.65 us (2%)
    pallas_call x1, Pallas kernels, local(): pl.pallas_call(functools.partial(kernel, counts, dims, near), out_shape=(...  29.3 us
    unnamed x7, local copies, waits for them, and re-layouts  2.87 us

profile of v1, /device:TPU:0, one launch (start us, length us, event | category | flops | bytes accessed | tf_op | source)
XLA Modules:
  0.0 32.8 jit_solution(1416850705965926559)
XLA Ops:
  0.6 29.3 %powers_basis.1 = (f32[2,4,8,8,128]{4,3,2,1,0:T(8,128)}, f32[9,9]{1,0:T(8,128)}, f32[1,9]{1,0:T(1,128)}) custom-call(f32[8,8,128]{2,1,0:T(8,128)} %res_ref.1, f32[8,8,128]{2,1,0:T(8,128)} %dir_ref.1), custom_call_target="tpu_custom_call" | custom-call | tf_op jit(solution)/shard_map/powers_basis/pallas_call | solution.py:483
  30.0 0.0 copy-start
  30.0 1.7 %copy.8 = f32[2,4,8,8,128]{4,3,2,1,0:T(8,128)} copy(f32[2,4,8,8,128]{4,3,2,1,0:T(8,128)} %get-tuple-element.12) | data formatting | bytes 524288
  31.7 0.0 copy-done
  31.7 0.0 copy-start.1
  31.7 0.6 %copy.9 = f32[9,9]{1,0:T(8,128)} copy(f32[9,9]{1,0:T(8,128)S(1)} %copy-done) | data formatting | bytes 648
  32.3 0.1 copy-done.1
  32.3 0.5 %copy.10 = f32[9]{0:T(128)} copy(f32[9]{0:T(128)S(1)} %bitcast.1) | data formatting | bytes 72
Async XLA Ops:
  30.0 1.7 %copy-start = (f32[9,9]{1,0:T(8,128)S(1)}, f32[9,9]{1,0:T(8,128)}, u32[]{:S(2)}) copy-start(f32[9,9]{1,0:T(8,128)} %get-tuple-element.13) | copy-start | bytes 976
  31.7 0.7 %copy-start.1 = (f32[1,9]{1,0:T(1,128)S(1)}, f32[1,9]{1,0:T(1,128)}, u32[]{:S(2)}) copy-start(f32[1,9]{1,0:T(1,128)} %get-tuple-element.8) | copy-start | bytes 112

commit v2 on v1

--- a/solution.py
+++ b/solution.py
@@ -36,7 +36,7 @@
 
 def kernel(
     counts, dims, near, res_ref, dir_ref, pow_ref, gram_ref, proj_ref,
-    main, pack, got, face, cbuf, czbuf, sbuf, szbuf, image, base, tab, ztab, t_ref, red0, red1,
+    main, pack, got, face, cbuf, czbuf, sbuf, szbuf, image, zsum, ubuf, tab, ztab, t_ref, red0, red1, spare,
     in_sem, out_sem, s_sem, r_sem, s0_sem, r0_sem, s1_sem, r1_sem,
 ):
     nx, ny, nz = counts
@@ -213,14 +213,22 @@
                     b = b * 0.5
                 parts.append(a + b)
             along_x = jnp.stack(parts)
-        extra = unpacked(z_src, xs)
-        up = rolled(jnp.where(last_lane[None], extra, mid), 1, 1)
-        down = rolled(jnp.where(first_lane[None], extra, mid), -1, 1)
         left, right = rolled(mid, 1, 0), rolled(mid, -1, 0)
         if weighted:
-            up, down = up * tab[UPZ][None], down * tab[DOWNZ][None]
             left, right = left * tab[UPY][None], right * tab[DOWNY][None]
-        return mid, (along_x + (left + right)) + (up + down)
+        return mid, (along_x + (left + right)) + zsum[pl.ds(lo, len(xs))]
+
+    def sweep_z(src, z_src, reach, weighted):
+        xs = list(range(-reach, cx + reach))
+        for x in xs:
+            ubuf[x + cx] = roll_lanes(z_src[(x + cx) // cx], -group * (x % cx))
+        for x in xs:
+            extra, mid = ubuf[x + cx], src[x + cx]
+            up = roll_lanes(jnp.where(last_lane, extra, mid), 1)
+            down = roll_lanes(jnp.where(first_lane, extra, mid), -1)
+            if weighted:
+                up, down = up * tab[UPZ], down * tab[DOWNZ]
+            zsum[x + cx] = up + down
 
     def z_beside(src, z_src, b, reach, weighted):
         mid = z_src[b]
@@ -247,6 +255,7 @@
 
     def apply_a(c, f, reach, index):
         src, z_src = main.at[c, f], pack.at[c, f]
+        sweep_z(src, z_src, reach, False)
         for xs in planes(reach):
             mid, around = beside(src, z_src, xs, False)
             value = 6.0 * mid - around
@@ -269,6 +278,7 @@
 
     def apply_m(c, f, reach):
         src, z_src = cbuf.at[c], czbuf.at[c]
+        sweep_z(src, z_src, reach + 1, True)
         for xs in planes(reach + 1):
             mid, around = beside(src, z_src, xs, True)
             sbuf[c, pl.ds(xs[0] + cx, len(xs))] = BETA * mid + around * table(lambda x: AM0 + (x + cx) // cx, xs)
@@ -276,6 +286,7 @@
             mid, around = z_beside(src, z_src, b, reach + 1, True)
             szbuf[c, b] = BETA * mid + around * ztab[ZAM + b]
         s_src, sz_src = sbuf.at[c], szbuf.at[c]
+        sweep_z(s_src, sz_src, reach, True)
         for xs in planes(reach):
             ds = pl.ds(xs[0] + cx, len(xs))
             _, around = beside(s_src, sz_src, xs, True)
@@ -302,7 +313,7 @@
             source = face.at[c, s]
             sink = got.at[c, s, 0 if dz > 0 else 1, 1 - dx, pl.ds(cy - cy * dy, cy)]
         return pltpu.make_async_remote_copy(
-            source, sink, s_sem.at[c, s, index], r_sem.at[c, s, index],
+            source, sink, s_sem.at[0], r_sem.at[c, s],
             device_id=target(OFFSETS[index]), device_id_type=MESH)
 
     def pack_face(c, s):
@@ -320,29 +331,39 @@
             def _():
                 copy_to(c, s, index).start()
 
+    around_it = [low[i].astype(jnp.int32) + high[i].astype(jnp.int32) for i in range(3)]
+    choices = [{1: (0,), 2: (1,)}.get(n, (1, 2)) for n in counts]
+
+    def tiles_of(c, s, ax, ay, az):
+        planes_in = ax * REACH[s][c] + ay * cx + ax * ay * (REACH[s][c] - 1)
+        return (planes_in + az * (1 + ax) * (1 + ay)) * (cy // 8)
+
+    def wait_bytes(sem, tiles):
+        view = spare.at[pl.ds(0, tiles)]
+        pltpu.make_async_copy(view, view, sem).wait()
+
+    def wait_exchanges(sem, pairs):
+        for ax in choices[0]:
+            for ay in choices[1]:
+                for az in choices[2]:
+                    here = (around_it[0] == ax) & (around_it[1] == ay) & (around_it[2] == az)
+                    tiles = sum(tiles_of(c, s, ax, ay, az) for c, s in pairs)
+                    if tiles:
+                        @pl.when(here)
+                        def _():
+                            wait_bytes(sem, tiles)
+
     def receive(c, s):
-        for index, offset in enumerate(OFFSETS):
-            @pl.when(exists(flip(offset)))
-            def _():
-                copy_to(c, s, index).wait_recv()
+        wait_exchanges(r_sem.at[c, s], [(c, s)])
         pack[c, 2 * s] = jnp.where(is_hi[None], got[c, s, 1], got[c, s, 0])
-
-    def done_sending(c, s):
-        for index, offset in enumerate(OFFSETS):
-            @pl.when(exists(offset))
-            def _():
-                copy_to(c, s, index).wait_send()
 
     def own(c, f):
         return main[c, f, pl.ds(cx, cx), pl.ds(cy, cy)].reshape(cx * cy, LANES)
 
-    outs = []
-
     def emit(c, f, slot_out):
         copy = pltpu.make_async_copy(
-            main.at[c, f, pl.ds(cx, cx), pl.ds(cy, cy)], pow_ref.at[c, slot_out], out_sem.at[c, slot_out])
+            main.at[c, f, pl.ds(cx, cx), pl.ds(cy, cy)], pow_ref.at[c, slot_out], out_sem.at[0])
         copy.start()
-        outs.append(copy)
 
     place_of = {a: (P_CHAIN, a) for a in range(STEPS + 1)}
     place_of.update({STEPS + 1 + k: (Z_CHAIN, k + 1) for k in range(STEPS)})
@@ -418,19 +439,21 @@
         jnp.ones((8, LANES), F32), t_ref[...], (((1,), (1,)), ((), ())),
         precision=HIGHEST, preferred_element_type=F32)[0:1]
 
-    def gather(value, axes, buffer, send_sem, recv_sem):
+    def gather(value, axes, buffer, send_sem, recv_sem, meanwhile=lambda: None):
         size, make = ahead(axes)
         buffer[0] = value
 
         def copy(k):
             return pltpu.make_async_remote_copy(
-                buffer.at[0], buffer.at[k], send_sem.at[k], recv_sem.at[k],
+                buffer.at[0], buffer.at[k], send_sem.at[0], recv_sem.at[0],
                 device_id=make(k), device_id_type=MESH)
 
         for k in range(1, size):
             copy(k).start()
-        for k in range(1, size):
-            copy(k).wait_recv()
+        meanwhile()
+        rest = buffer.at[pl.ds(1, size - 1)]
+        pltpu.make_async_copy(rest, rest, send_sem.at[0]).wait()
+        pltpu.make_async_copy(rest, rest, recv_sem.at[0]).wait()
         result = jnp.zeros_like(value)
         for k in range(size):
             rest, at = k, 0
@@ -441,24 +464,21 @@
                 at = at + scale * lax.rem(place[AXES.index(a)] + n - want, n)
                 scale *= n
             result = result + buffer[at]
-        for k in range(1, size):
-            copy(k).wait_send()
         return result
 
+    def finish():
+        wait_exchanges(s_sem.at[0], [(c, s) for c in (0, 1) for s in (0, 1)])
+        wait_bytes(out_sem.at[0], 2 * STEPS * cx * (cy // 8))
+
     if near:
-        value = gather(value, AXES, red0, s0_sem, r0_sem)
+        value = gather(value, AXES, red0, s0_sem, r0_sem, finish)
     else:
-        value = gather(value, ("gy", "gz"), red0, s0_sem, r0_sem)
+        value = gather(value, ("gy", "gz"), red0, s0_sem, r0_sem, finish)
         value = gather(value, ("gx",), red1, s1_sem, r1_sem)
     value = value * (1.0 / (nx * cx * ny * cy * nz * cz))
     for a in range(total):
         gram_ref[a:a + 1, :] = value[0:1, a * total:(a + 1) * total]
     proj_ref[...] = value[0:1, total * total:total * total + total]
-    for c in (0, 1):
-        for s in (0, 1):
-            done_sending(c, s)
-    for copy in outs:
-        copy.wait()
 
 
 def solution(mesh):
@@ -479,7 +499,6 @@
         hbm = pl.BlockSpec(memory_space=pl.ANY)
         ext = (3 * cx, 3 * cy, LANES)
         zext = (3, 3 * cy, LANES)
-        n = len(OFFSETS)
         powers, gram, proj = pl.pallas_call(
             functools.partial(kernel, counts, dims, near),
             out_shape=(
@@ -499,16 +518,18 @@
                 pltpu.VMEM((2,) + ext, F32),
                 pltpu.VMEM((2,) + zext, F32),
                 pltpu.VMEM((total, cx, cy, LANES), F32),
-                pltpu.VMEM((1, 8, LANES), F32),
+                pltpu.VMEM(ext, F32),
+                pltpu.VMEM(ext, F32),
                 pltpu.VMEM((22, 3 * cy, LANES), F32),
                 pltpu.VMEM((20, 3 * cy, LANES), F32),
                 pltpu.VMEM((LANES, LANES), F32),
                 pltpu.VMEM((plane, 1, LANES), F32),
                 pltpu.VMEM((counts[0], 1, LANES), F32),
-                dma((2,)), dma((2, STEPS)),
-                dma((2, 2, n)), dma((2, 2, n)),
-                dma((plane,)), dma((plane,)),
-                dma((counts[0],)), dma((counts[0],)),
+                pltpu.VMEM((4 * 9 * cx * (cy // 8), 8, LANES), F32),
+                dma((2,)), dma((1,)),
+                dma((1,)), dma((2, 2)),
+                dma((1,)), dma((1,)),
+                dma((1,)), dma((1,)),
             ],
             compiler_params=pltpu.CompilerParams(collective_id=0, has_side_effects=True),
             name="powers_basis",

time: 33.1 us -> 28.5 us (0.86)
  Pallas kernels: 29.3 us -> 24.8 us
    pallas_call x1, Pallas kernels: 29.3 us -> 24.8 us  [local(): pl.pallas_call(functools.partial(kernel, counts, dims, near), out_shape=(...]
where the time goes in v2:
time: 28.5 us; the launch traced here: 28.3 us
  Pallas kernels  24.8 us (87%)
  local copies, waits for them, and re-layouts  2.87 us (10%)
  between operations  0.65 us (2%)
    pallas_call x1, Pallas kernels, local(): pl.pallas_call(functools.partial(kernel, counts, dims, near), out_shape=(...  24.8 us
    unnamed x7, local copies, waits for them, and re-layouts  2.87 us

profile of v2, /device:TPU:0, one launch (start us, length us, event | category | flops | bytes accessed | tf_op | source)
XLA Modules:
  0.0 28.3 jit_solution(3286495152436815428)
XLA Ops:
  0.6 24.8 %powers_basis.1 = (f32[2,4,8,8,128]{4,3,2,1,0:T(8,128)}, f32[9,9]{1,0:T(8,128)}, f32[1,9]{1,0:T(1,128)}) custom-call(f32[8,8,128]{2,1,0:T(8,128)} %res_ref.1, f32[8,8,128]{2,1,0:T(8,128)} %dir_ref.1), custom_call_target="tpu_custom_call" | custom-call | tf_op jit(solution)/shard_map/powers_basis/pallas_call | solution.py:502
  25.5 0.0 copy-start
  25.5 1.7 %copy.8 = f32[2,4,8,8,128]{4,3,2,1,0:T(8,128)} copy(f32[2,4,8,8,128]{4,3,2,1,0:T(8,128)} %get-tuple-element.12) | data formatting | bytes 524288
  27.1 0.0 copy-done
  27.1 0.0 copy-start.1
  27.1 0.6 %copy.9 = f32[9,9]{1,0:T(8,128)} copy(f32[9,9]{1,0:T(8,128)S(1)} %copy-done) | data formatting | bytes 648
  27.7 0.1 copy-done.1
  27.8 0.5 %copy.10 = f32[9]{0:T(128)} copy(f32[9]{0:T(128)S(1)} %bitcast.1) | data formatting | bytes 72
Async XLA Ops:
  25.5 1.7 %copy-start = (f32[9,9]{1,0:T(8,128)S(1)}, f32[9,9]{1,0:T(8,128)}, u32[]{:S(2)}) copy-start(f32[9,9]{1,0:T(8,128)} %get-tuple-element.13) | copy-start | bytes 976
  27.1 0.7 %copy-start.1 = (f32[1,9]{1,0:T(1,128)S(1)}, f32[1,9]{1,0:T(1,128)}, u32[]{:S(2)}) copy-start(f32[1,9]{1,0:T(1,128)} %get-tuple-element.8) | copy-start | bytes 112

commit v3 on v2

--- a/solution.py
+++ b/solution.py
@@ -17,6 +17,7 @@
 P_CHAIN, Z_CHAIN = 0, 1
 REACH = ((6, 5), (7, 7))
 CHUNK = 4
+RUN = 4
 OFFSETS = [(dx, dy, dz) for dx in (-1, 0, 1) for dy in (-1, 0, 1) for dz in (-1, 0, 1) if (dx, dy, dz) != (0, 0, 0)]
 
 
@@ -36,7 +37,7 @@
 
 def kernel(
     counts, dims, near, res_ref, dir_ref, pow_ref, gram_ref, proj_ref,
-    main, pack, got, face, cbuf, czbuf, sbuf, szbuf, image, zsum, ubuf, tab, ztab, t_ref, red0, red1, spare,
+    raw, main, pack, got, face, flat, cbuf, czbuf, sbuf, szbuf, image, zsum, zzsum, tab, ztab, up_tab, down_tab, d_tab, g_tab, t_ref, red0, red1, spare,
     in_sem, out_sem, s_sem, r_sem, s0_sem, r0_sem, s1_sem, r1_sem,
 ):
     nx, ny, nz = counts
@@ -78,7 +79,7 @@
         return size, make
 
     loads = [
-        pltpu.make_async_copy(ref, main.at[c, 0, pl.ds(cx, cx), pl.ds(cy, cy)], in_sem.at[c])
+        pltpu.make_async_copy(ref, raw.at[c, 0, pl.ds(cx, cx), pl.ds(cy, cy)], in_sem.at[c])
         for c, ref in ((Z_CHAIN, res_ref), (P_CHAIN, dir_ref))
     ]
     for copy in loads:
@@ -98,7 +99,7 @@
                 pl.semaphore_signal(barrier, 1, device_id=make(k), device_id_type=MESH)
             expected = expected + (size - 1)
 
-    fields = [(c, f) for c in (0, 1) for f in (0, 2)]
+    fields = [(c, f) for c in (0, 1) for f in (0, 1)]
     for flag, xs, ys in (
         (low[0], pl.ds(0, cx), pl.ds(0, rows)), (high[0], pl.ds(2 * cx, cx), pl.ds(0, rows)),
         (low[1], pl.ds(0, 3 * cx), pl.ds(0, cy)), (high[1], pl.ds(0, 3 * cx), pl.ds(2 * cy, cy)),
@@ -106,7 +107,7 @@
         @pl.when(jnp.logical_not(flag))
         def _():
             for c, f in fields:
-                main[c, f, xs, ys] = jnp.zeros((xs.size, ys.size, LANES), F32)
+                raw[c, f, xs, ys] = jnp.zeros((xs.size, ys.size, LANES), F32)
     for flag, ss, xs, ys in (
         (low[2], 0, pl.ds(0, 3), pl.ds(0, rows)), (high[2], 1, pl.ds(0, 3), pl.ds(0, rows)),
         (low[0], None, pl.ds(0, 1), pl.ds(0, rows)), (high[0], None, pl.ds(2, 1), pl.ds(0, rows)),
@@ -127,18 +128,27 @@
     def x_terms(x):
         return axis_terms(jnp.int32(x), cx, low[0], high[0], gx, nx)
 
-    D_REPS = (-3, -1, 0, 3, cx - 1, cx, cx + 2)
-    D0, AM0, M0, G0, UPY, DOWNY, UPZ, DOWNZ = 0, 7, 10, 13, 18, 19, 20, 21
-    wyz, myz, fyz = wy * wz, my * mz, fy + fz
-    for k, x in enumerate(D_REPS):
-        tab[D0 + k] = wyz * x_terms(x)[0]
+    AM0, M0, UPY, DOWNY = 0, 3, 6, 7
+    wyz, myz, gyz = wy * wz, my * mz, GAMMA + DELTA * (fy + fz)
     for k, x in enumerate((-3, 3, cx + 2)):
         mask = myz * x_terms(x)[4]
         tab[AM0 + k] = mask * ALPHA
         tab[M0 + k] = mask
-    for k, x in enumerate((3, -2, 1, cx - 2, cx + 1)):
-        tab[G0 + k] = GAMMA + DELTA * (fyz + x_terms(x)[1])
-    tab[UPY], tab[DOWNY], tab[UPZ], tab[DOWNZ] = up_y, down_y, up_z, down_z
+    tab[UPY], tab[DOWNY] = up_y, down_y
+    runs = 3 * cx // RUN
+
+    def turn(x):
+        return group * ((x + cx) // RUN)
+
+    for g in range(runs):
+        up_tab[g] = pltpu.roll(up_z[:cy], group * g, 1) if g else up_z[:cy]
+        down_tab[g] = pltpu.roll(down_z[:cy], group * g, 1) if g else down_z[:cy]
+        d_run = pltpu.roll(wyz, group * g, 1) if g else wyz
+        g_run = pltpu.roll(gyz, group * g, 1) if g else gyz
+        for k in range(RUN * g, RUN * g + RUN):
+            cover, inner = x_terms(k - cx)[:2]
+            d_tab[k] = d_run * cover
+            g_tab[k] = g_run + DELTA * inner
     below_1, above_6 = x_terms(1)[2], x_terms(cx - 2)[3]
 
     slot = (lane + half) // group % cx
@@ -146,9 +156,10 @@
     is_hi = deep >= 0
     z_at = jnp.where(is_hi, deep + cz, deep)
     wzz, fzz, up_zz, down_zz, mzz = axis_terms(z_at, cz, low[2], high[2], gz, nz)
-    ZD, ZAM, ZM, ZG, ZUX, ZDX, ZUZ, ZDZ = 0, 3, 6, 9, 12, 15, 18, 19
-    for b in range(3):
-        wx, fx, up_x, down_x, mx = axis_terms(slot + (b - 1) * cx, cx, low[0], high[0], gx, nx)
+    ZD, ZAM, ZM, ZG, ZUX, ZDX = (RUN * k for k in range(6))
+    ZUZ, ZDZ = 6 * RUN, 6 * RUN + 1
+    for b in range(RUN):
+        wx, fx, up_x, down_x, mx = axis_terms(slot * RUN + (b - cx), cx, low[0], high[0], gx, nx)
         ztab[ZD + b] = wx * wy * wzz
         ztab[ZAM + b] = mx * my * mzz * ALPHA
         ztab[ZM + b] = mx * my * mzz
@@ -156,19 +167,10 @@
         ztab[ZUX + b] = up_x
         ztab[ZDX + b] = down_x
     ztab[ZUZ], ztab[ZDZ] = up_zz, down_zz
-    first_lane, last_lane = lane == 0, lane == LANES - 1
     at_first, at_last = deep == 0, deep == -1
-    first_slot, last_slot = slot == 0, slot == cx - 1
-
-    def d_class(x):
-        if x < 0:
-            return D0 + (1 if x == -1 else 0)
-        if x >= cx:
-            return D0 + (5 if x == cx else 6)
-        return D0 + (2 if x == 0 else 4 if x == cx - 1 else 3)
-
-    def g_class(x):
-        return G0 + {-2: 1, 1: 2, cx - 2: 3, cx + 1: 4}.get(x, 0)
+    is_first = [lane == group * g for g in range(runs)]
+    is_last = [lane == (group * g - 1) % LANES for g in range(runs)]
+    is_edge = [is_first[g] | is_last[g] for g in range(runs)]
 
     def roll_rows(v, shift):
         return pltpu.roll(v, shift % v.shape[0], 0)
@@ -185,130 +187,149 @@
         xs = list(range(-reach, cx + reach))
         return [xs[i:i + CHUNK] for i in range(0, len(xs), CHUNK)]
 
-    def table(kind, xs):
-        ks = [kind(x) for x in xs]
+    def table(at, xs):
+        ks = [at + (x + cx) // cx for x in xs]
         if len(set(ks)) == 1:
             return tab[ks[0]][None]
         return jnp.stack([tab[k] for k in ks])
 
-    def unpacked(z_src, xs):
-        return jnp.stack([roll_lanes(z_src[(x + cx) // cx], -group * (x % cx)) for x in xs])
-
-    def beside(src, z_src, xs, weighted):
+    def thrice(v):
+        return jnp.concatenate([v] * 3, axis=0)
+
+    flips = [0]
+
+    def stream(src, z_src, reach, weighted):
+        flips[0] ^= 1
+        out, z_out = zsum.at[flips[0]], zzsum.at[flips[0]]
+        for b in range(RUN):
+            mid = z_src[b]
+            inject = jnp.zeros((rows, LANES), F32)
+            for g in range(runs):
+                x = g * RUN + b - cx
+                if -reach <= x < cx + reach:
+                    inject = jnp.where(is_edge[g], src[x + cx], inject)
+            up = roll_lanes(jnp.where(at_last, inject, mid), 1)
+            down = roll_lanes(jnp.where(at_first, inject, mid), -1)
+            if weighted:
+                up, down = up * ztab[ZUZ], down * ztab[ZDZ]
+            part = up + down
+            if b == 0:
+                before = roll_lanes(z_src[RUN - 1], group)
+                part = part + (before * ztab[ZUX] if weighted else before)
+            if b == RUN - 1:
+                after = roll_lanes(z_src[0], -group)
+                part = part + (after * ztab[ZDX + b] if weighted else after)
+            z_out[b] = part
+        for x in range(-reach, cx + reach):
+            g, b = divmod(x + cx, RUN)
+            mid, extra = src[x + cx], z_src[b]
+            up = roll_lanes(jnp.where(is_last[g], extra, mid), 1)
+            down = roll_lanes(jnp.where(is_first[g], extra, mid), -1)
+            if weighted:
+                up, down = up * thrice(up_tab[g]), down * thrice(down_tab[g])
+            part = up + down
+            if b == 0:
+                part = part + roll_lanes(src[x + cx - 1], group)
+            if b == RUN - 1:
+                part = part + roll_lanes(src[x + cx + 1], -group)
+            out[x + cx] = part
+        return out, z_out
+
+    def beside(src, sums, xs, weighted):
         lo = xs[0] + cx
         mid = src[pl.ds(lo, len(xs))]
-        if not weighted or not set(xs) & {1, cx - 2, -2, cx + 1}:
-            along_x = src[pl.ds(lo - 1, len(xs))] + src[pl.ds(lo + 1, len(xs))]
-        else:
-            parts = []
-            for x in xs:
-                a, b = src[x + cx - 1], src[x + cx + 1]
-                if x == 1:
-                    a = a * below_1
-                if x == cx + 1:
-                    a = a * 0.5
-                if x == cx - 2:
-                    b = b * above_6
-                if x == -2:
-                    b = b * 0.5
-                parts.append(a + b)
-            along_x = jnp.stack(parts)
+        parts = []
+        for x in xs:
+            b = (x + cx) % RUN
+            part = sums[x + cx]
+            if b > 0:
+                value = src[x + cx - 1]
+                if weighted and x == 1:
+                    value = value * below_1
+                if weighted and x == cx + 1:
+                    value = value * 0.5
+                part = part + value
+            if b < RUN - 1:
+                value = src[x + cx + 1]
+                if weighted and x == cx - 2:
+                    value = value * above_6
+                if weighted and x == -2:
+                    value = value * 0.5
+                part = part + value
+            parts.append(part)
         left, right = rolled(mid, 1, 0), rolled(mid, -1, 0)
         if weighted:
             left, right = left * tab[UPY][None], right * tab[DOWNY][None]
-        return mid, (along_x + (left + right)) + zsum[pl.ds(lo, len(xs))]
-
-    def sweep_z(src, z_src, reach, weighted):
-        xs = list(range(-reach, cx + reach))
-        for x in xs:
-            ubuf[x + cx] = roll_lanes(z_src[(x + cx) // cx], -group * (x % cx))
-        for x in xs:
-            extra, mid = ubuf[x + cx], src[x + cx]
-            up = roll_lanes(jnp.where(last_lane, extra, mid), 1)
-            down = roll_lanes(jnp.where(first_lane, extra, mid), -1)
-            if weighted:
-                up, down = up * tab[UPZ], down * tab[DOWNZ]
-            zsum[x + cx] = up + down
-
-    def z_beside(src, z_src, b, reach, weighted):
+        return mid, jnp.stack(parts) + (left + right)
+
+    def z_beside(z_src, z_sums, b, weighted):
         mid = z_src[b]
-        inject = jnp.zeros((rows, LANES), F32)
-        for g in range(cx):
-            x = g + (b - 1) * cx
-            if -reach <= x < cx + reach:
-                inject = jnp.where(slot_edge[g], roll_lanes(src[x + cx], group * g), inject)
-        up = roll_lanes(jnp.where(at_last, inject, mid), 1)
-        down = roll_lanes(jnp.where(at_first, inject, mid), -1)
         left, right = roll_rows(mid, 1), roll_rows(mid, -1)
-        before, after = roll_lanes(mid, group), roll_lanes(mid, -group)
+        if weighted:
+            left, right = left * tab[UPY], right * tab[DOWNY]
+        around = z_sums[b] + (left + right)
         if b > 0:
-            before = jnp.where(first_slot, roll_lanes(z_src[b - 1], group), before)
-        if b < 2:
-            after = jnp.where(last_slot, roll_lanes(z_src[b + 1], -group), after)
-        if weighted:
-            up, down = up * ztab[ZUZ], down * ztab[ZDZ]
-            left, right = left * tab[UPY], right * tab[DOWNY]
-            before, after = before * ztab[ZUX + b], after * ztab[ZDX + b]
-        return mid, ((before + after) + (left + right)) + (up + down)
-
-    slot_edge = [(slot == g) & ((deep == 0) | (deep == -1)) for g in range(cx)]
+            around = around + (z_src[b - 1] * ztab[ZUX + b] if weighted else z_src[b - 1])
+        if b < RUN - 1:
+            around = around + (z_src[b + 1] * ztab[ZDX + b] if weighted else z_src[b + 1])
+        return mid, around
 
     def apply_a(c, f, reach, index):
         src, z_src = main.at[c, f], pack.at[c, f]
-        sweep_z(src, z_src, reach, False)
+        sums, z_sums = stream(src, z_src, reach, False)
+        if reach > 0:
+            for b in range(RUN):
+                mid, around = z_beside(z_src, z_sums, b, False)
+                czbuf[c, b] = (6.0 * mid - around) * ztab[ZD + b]
         for xs in planes(reach):
-            mid, around = beside(src, z_src, xs, False)
+            mid, around = beside(src, sums, xs, False)
             value = 6.0 * mid - around
             for i, x in enumerate(xs):
                 if 0 <= x < cx:
                     image[index, x] = value[i, cy:2 * cy]
             if reach > 0:
-                cbuf[c, pl.ds(xs[0] + cx, len(xs))] = value * table(d_class, xs)
-        if reach > 0:
-            for b in range(3):
-                mid, around = z_beside(src, z_src, b, reach, False)
-                czbuf[c, b] = (6.0 * mid - around) * ztab[ZD + b]
+                ds = pl.ds(xs[0] + cx, len(xs))
+                cbuf[c, ds] = value * d_tab[ds]
 
     def scale_only(c, f, reach):
+        for b in range(RUN):
+            czbuf[c, b] = pack[c, f, b] * ztab[ZD + b]
         for xs in planes(reach):
             ds = pl.ds(xs[0] + cx, len(xs))
-            cbuf[c, ds] = main[c, f, ds] * table(d_class, xs)
-        for b in range(3):
-            czbuf[c, b] = pack[c, f, b] * ztab[ZD + b]
+            cbuf[c, ds] = main[c, f, ds] * d_tab[ds]
 
     def apply_m(c, f, reach):
         src, z_src = cbuf.at[c], czbuf.at[c]
-        sweep_z(src, z_src, reach + 1, True)
+        sums, z_sums = stream(src, z_src, reach + 1, True)
+        for b in range(RUN):
+            mid, around = z_beside(z_src, z_sums, b, True)
+            szbuf[c, b] = BETA * mid + around * ztab[ZAM + b]
         for xs in planes(reach + 1):
-            mid, around = beside(src, z_src, xs, True)
-            sbuf[c, pl.ds(xs[0] + cx, len(xs))] = BETA * mid + around * table(lambda x: AM0 + (x + cx) // cx, xs)
-        for b in range(3):
-            mid, around = z_beside(src, z_src, b, reach + 1, True)
-            szbuf[c, b] = BETA * mid + around * ztab[ZAM + b]
+            mid, around = beside(src, sums, xs, True)
+            sbuf[c, pl.ds(xs[0] + cx, len(xs))] = BETA * mid + around * table(AM0, xs)
         s_src, sz_src = sbuf.at[c], szbuf.at[c]
-        sweep_z(s_src, sz_src, reach, True)
+        sums, z_sums = stream(s_src, sz_src, reach, True)
+        if reach > 0:
+            for b in range(RUN):
+                _, around = z_beside(sz_src, z_sums, b, True)
+                pack[c, f, b] = z_src[b] * ztab[ZG + b] + around * ztab[ZM + b]
         for xs in planes(reach):
             ds = pl.ds(xs[0] + cx, len(xs))
-            _, around = beside(s_src, sz_src, xs, True)
-            value = src[ds] * table(g_class, xs)
+            _, around = beside(s_src, sums, xs, True)
+            value = src[ds] * g_tab[ds]
             if reach > 0:
-                main[c, f, ds] = value + around * table(lambda x: M0 + (x + cx) // cx, xs)
+                main[c, f, ds] = value + around * table(M0, xs)
             else:
                 main[c, f, ds, pl.ds(cy, cy)] = (value + around)[:, cy:2 * cy]
-        if reach > 0:
-            for b in range(3):
-                _, around = z_beside(s_src, sz_src, b, reach, True)
-                pack[c, f, b] = z_src[b] * ztab[ZG + b] + around * ztab[ZM + b]
 
     def copy_to(c, s, index):
         dx, dy, dz = OFFSETS[index]
-        f = 2 * s
         if dz == 0:
             n = cx if dx == 0 else REACH[s][c] - (dy != 0)
             first = cx if dx <= 0 else 2 * cx - n
             there = pl.ds(first - cx * dx, n)
-            source = main.at[c, f, pl.ds(first, n), pl.ds(cy, cy)]
-            sink = main.at[c, f, there, pl.ds(cy - cy * dy, cy)]
+            source = raw.at[c, s, pl.ds(first, n), pl.ds(cy, cy)]
+            sink = raw.at[c, s, there, pl.ds(cy - cy * dy, cy)]
         else:
             source = face.at[c, s]
             sink = got.at[c, s, 0 if dz > 0 else 1, 1 - dx, pl.ds(cy - cy * dy, cy)]
@@ -316,13 +337,26 @@
             source, sink, s_sem.at[0], r_sem.at[c, s],
             device_id=target(OFFSETS[index]), device_id_type=MESH)
 
+    per_block = cx // RUN
+
     def pack_face(c, s):
-        f = 2 * s
         value = jnp.zeros((cy, LANES), F32)
-        for g in range(cx):
-            moved = roll_lanes(main[c, f, cx + g, pl.ds(cy, cy)], group * g)
-            value = jnp.where(slot[:cy] == g, moved, value)
+        for i in range(RUN):
+            joined = main[c, 2 * s, cx + i, pl.ds(cy, cy)]
+            for h in range(1, per_block):
+                other = main[c, 2 * s, cx + h * RUN + i, pl.ds(cy, cy)]
+                joined = jnp.where(slot[:cy] == per_block + h, other, joined)
+            moved = roll_lanes(joined, group * (per_block * i - per_block))
+            value = jnp.where(slot[:cy] // per_block == i, moved, value)
         face[c, s] = value
+
+    def turn_own(c):
+        for x in range(cx):
+            main[c, 0, x + cx, pl.ds(cy, cy)] = roll_lanes(raw[c, 0, x + cx, pl.ds(cy, cy)], turn(x))
+
+    def turn_back(c, f, out):
+        for x in range(cx):
+            out[x] = roll_lanes(main[c, f, x + cx, pl.ds(cy, cy)], -turn(x))
 
     def send(c, s):
         order = sorted(range(len(OFFSETS)), key=lambda i: -sum(abs(v) for v in OFFSETS[i]))
@@ -355,15 +389,26 @@
 
     def receive(c, s):
         wait_exchanges(r_sem.at[c, s], [(c, s)])
-        pack[c, 2 * s] = jnp.where(is_hi[None], got[c, s, 1], got[c, s, 0])
+        f = 2 * s
+        faces = [jnp.where(is_hi, got[c, s, 1, k], got[c, s, 0, k]) for k in range(3)]
+        for b in range(RUN):
+            value = jnp.zeros((rows, LANES), F32)
+            for k in range(3):
+                moved = roll_lanes(faces[k], group * per_block * (k - b))
+                value = jnp.where(slot // per_block == k, moved, value)
+            pack[c, f, b] = value
+        for x in range(-REACH[s][c], cx + REACH[s][c]):
+            if 0 <= x < cx:
+                for y in (0, 2 * cy):
+                    main[c, f, x + cx, pl.ds(y, cy)] = roll_lanes(raw[c, s, x + cx, pl.ds(y, cy)], turn(x))
+            else:
+                main[c, f, x + cx] = roll_lanes(raw[c, s, x + cx], turn(x))
 
     def own(c, f):
         return main[c, f, pl.ds(cx, cx), pl.ds(cy, cy)].reshape(cx * cy, LANES)
 
     def emit(c, f, slot_out):
-        copy = pltpu.make_async_copy(
-            main.at[c, f, pl.ds(cx, cx), pl.ds(cy, cy)], pow_ref.at[c, slot_out], out_sem.at[0])
-        copy.start()
+        turn_back(c, f, pow_ref.at[c, slot_out])
 
     place_of = {a: (P_CHAIN, a) for a in range(STEPS + 1)}
     place_of.update({STEPS + 1 + k: (Z_CHAIN, k + 1) for k in range(STEPS)})
@@ -384,6 +429,7 @@
     for copy in loads:
         copy.wait()
     for c in (Z_CHAIN, P_CHAIN):
+        turn_own(c)
         pack_face(c, 0)
     pl.semaphore_wait(barrier, expected)
     send(Z_CHAIN, 0)
@@ -396,6 +442,7 @@
     emit(Z_CHAIN, 1, 0)
     apply_a(Z_CHAIN, 1, 2, first_z)
     apply_m(Z_CHAIN, 2, 0)
+    turn_back(Z_CHAIN, 2, raw.at[Z_CHAIN, 1, pl.ds(cx, cx), pl.ds(cy, cy)])
     pack_face(Z_CHAIN, 1)
     send(Z_CHAIN, 1)
     emit(Z_CHAIN, 2, 1)
@@ -406,6 +453,7 @@
     emit(P_CHAIN, 1, 0)
     apply_a(P_CHAIN, 1, 2, 1)
     apply_m(P_CHAIN, 2, 0)
+    turn_back(P_CHAIN, 2, raw.at[P_CHAIN, 1, pl.ds(cx, cx), pl.ds(cy, cy)])
     pack_face(P_CHAIN, 1)
     send(P_CHAIN, 1)
     emit(P_CHAIN, 2, 1)
@@ -468,7 +516,6 @@
 
     def finish():
         wait_exchanges(s_sem.at[0], [(c, s) for c in (0, 1) for s in (0, 1)])
-        wait_bytes(out_sem.at[0], 2 * STEPS * cx * (cy // 8))
 
     if near:
         value = gather(value, AXES, red0, s0_sem, r0_sem, finish)
@@ -481,6 +528,15 @@
     proj_ref[...] = value[0:1, total * total:total * total + total]
 
 
+def store(pow_ref, gram_ref, proj_ref, pow_out, gram_out, proj_out, sem):
+    pairs = ((pow_ref, pow_out), (gram_ref, gram_out), (proj_ref, proj_out))
+    copies = [pltpu.make_async_copy(a, b, sem.at[i]) for i, (a, b) in enumerate(pairs)]
+    for copy in copies:
+        copy.start()
+    for copy in copies:
+        copy.wait()
+
+
 def solution(mesh):
     counts = tuple(mesh.shape[a] for a in AXES)
     near = max(counts) <= 4
@@ -496,9 +552,9 @@
         fields = STEPS + 1
         dma = pltpu.SemaphoreType.DMA
         vm = pl.BlockSpec(memory_space=pltpu.VMEM)
-        hbm = pl.BlockSpec(memory_space=pl.ANY)
+        hbm = pl.BlockSpec(memory_space=pltpu.HBM)
         ext = (3 * cx, 3 * cy, LANES)
-        zext = (3, 3 * cy, LANES)
+        zext = (RUN, 3 * cy, LANES)
         powers, gram, proj = pl.pallas_call(
             functools.partial(kernel, counts, dims, near),
             out_shape=(
@@ -507,21 +563,27 @@
                 jax.ShapeDtypeStruct((1, total), F32),
             ),
             in_specs=[hbm, hbm],
-            out_specs=(hbm, vm, vm),
+            out_specs=(vm, vm, vm),
             scratch_shapes=[
+                pltpu.VMEM((2, 2) + ext, F32),
                 pltpu.VMEM((2, fields) + ext, F32),
                 pltpu.VMEM((2, fields) + zext, F32),
-                pltpu.VMEM((2, 2, 2) + zext, F32),
+                pltpu.VMEM((2, 2, 2, 3, 3 * cy, LANES), F32),
                 pltpu.VMEM((2, 2, cy, LANES), F32),
+                pltpu.VMEM((2, STEPS) + dims, F32),
                 pltpu.VMEM((2,) + ext, F32),
                 pltpu.VMEM((2,) + zext, F32),
                 pltpu.VMEM((2,) + ext, F32),
                 pltpu.VMEM((2,) + zext, F32),
-                pltpu.VMEM((total, cx, cy, LANES), F32),
+                pltpu.VMEM((total,) + dims, F32),
+                pltpu.VMEM((2,) + ext, F32),
+                pltpu.VMEM((2,) + zext, F32),
+                pltpu.VMEM((8, 3 * cy, LANES), F32),
+                pltpu.VMEM((6 * RUN + 2, 3 * cy, LANES), F32),
+                pltpu.VMEM((3 * cx // RUN, cy, LANES), F32),
+                pltpu.VMEM((3 * cx // RUN, cy, LANES), F32),
                 pltpu.VMEM(ext, F32),
                 pltpu.VMEM(ext, F32),
-                pltpu.VMEM((22, 3 * cy, LANES), F32),
-                pltpu.VMEM((20, 3 * cy, LANES), F32),
                 pltpu.VMEM((LANES, LANES), F32),
                 pltpu.VMEM((plane, 1, LANES), F32),
                 pltpu.VMEM((counts[0], 1, LANES), F32),
@@ -531,9 +593,22 @@
                 dma((1,)), dma((1,)),
                 dma((1,)), dma((1,)),
             ],
-            compiler_params=pltpu.CompilerParams(collective_id=0, has_side_effects=True),
+            compiler_params=pltpu.CompilerParams(collective_id=0, has_side_effects=True, vmem_limit_bytes=24 << 20),
             name="powers_basis",
-        )(residual, direction)
+        )(*[pltpu.with_memory_space_constraint(v, pltpu.HBM) for v in (residual, direction)])
+        powers, gram, proj = pl.pallas_call(
+            store,
+            out_shape=(
+                jax.ShapeDtypeStruct((2, STEPS) + dims, F32),
+                jax.ShapeDtypeStruct((total, total), F32),
+                jax.ShapeDtypeStruct((1, total), F32),
+            ),
+            in_specs=[vm, vm, vm],
+            out_specs=(hbm, hbm, hbm),
+            scratch_shapes=[dma((3,))],
+            compiler_params=pltpu.CompilerParams(vmem_limit_bytes=1 << 20),
+            name="store",
+        )(powers, gram, proj)
         return powers, gram, proj.reshape(total)
 
     placed = (P("gx", "gy", "gz"), P("gx", "gy", "gz"))

time: 28.5 us -> 23.4 us (0.82)
  local copies, waits for them, and re-layouts: 2.87 us -> 0 us
  Pallas kernels: 24.8 us -> 22.5 us
    pallas_call x1, Pallas kernels: 24.8 us -> 21.8 us  [local(): pl.pallas_call(functools.partial(kernel, counts, dims, near), out_shape=(...]
    unnamed x7 -> x0, local copies, waits for them, and re-layouts: 2.87 us -> none
    pallas_call x0 -> x1, Pallas kernels: none -> 0.74 us  [local(): pl.pallas_call(store, out_shape=(jax.ShapeDtypeStruct((2, STEPS) + dims,...]
where the time goes in v3:
time: 23.4 us; the launch traced here: 23.2 us
  Pallas kernels  22.5 us (96%)
  between operations  0.64 us (3%)
    pallas_call x1, Pallas kernels, local(): pl.pallas_call(functools.partial(kernel, counts, dims, near), out_shape=(...  21.8 us
    pallas_call x1, Pallas kernels, local(): pl.pallas_call(store, out_shape=(jax.ShapeDtypeStruct((2, STEPS) + dims,...  0.74 us

profile of v3, /device:TPU:0, one launch (start us, length us, event | category | flops | bytes accessed | tf_op | source)
XLA Modules:
  0.0 23.2 jit_solution(6664697970273887610)
XLA Ops:
  0.6 21.8 %powers_basis.1 = (f32[2,4,8,8,128]{4,3,2,1,0:T(8,128)S(1)}, f32[9,9]{1,0:T(8,128)S(1)}, f32[1,9]{1,0:T(1,128)S(1)}) custom-call(f32[8,8,128]{2,1,0:T(8,128)} %res_ref.1, f32[8,8,128]{2,1,0:T(8,128)} %dir_ref.1), custom_call_target="tpu_custom_call" | custom-call | tf_op jit(solution)/shard_map/powers_basis/pallas_call | solution.py:558
  22.4 0.7 %store.1 = (f32[2,4,8,8,128]{4,3,2,1,0:T(8,128)}, f32[9,9]{1,0:T(8,128)}, f32[1,9]{1,0:T(1,128)}) custom-call(f32[2,4,8,8,128]{4,3,2,1,0:T(8,128)S(1)} %get-tuple-element.9.pow_ref, f32[9,9]{1,0:T(8,128)S(1)} %get-tuple-element.10.gram_ref, f32[1,9]{1,0:T(1,128)S(1)} %get-tuple-element.11.proj_ref), custom_call_target="tpu_custom_call" | custom-call | tf_op jit(solution)/shard_map/store/pallas_call | solution.py:599

commit v4 on v3

v4 whole, which is shorter than its diff:
```python
import functools

import jax
import jax.numpy as jnp
from jax import lax
from jax.experimental import pallas as pl
from jax.experimental.pallas import tpu as pltpu
from jax.sharding import PartitionSpec as P

STEPS = 4
LANES = 128
MESH = pl.DeviceIdType.MESH
HIGHEST = lax.Precision.HIGHEST
F32 = jnp.float32
AXES = ("gx", "gy", "gz")
GAMMA, BETA, ALPHA, DELTA = 13.0 / 81.0, 5.0 / 243.0, 1.0 / 729.0, 1.0 / 1458.0
P_CHAIN, Z_CHAIN = 0, 1
REACH = ((6, 5), (7, 7))
CHUNK = 4
RUN = 4
OFFSETS = [(dx, dy, dz) for dx in (-1, 0, 1) for dy in (-1, 0, 1) for dz in (-1, 0, 1) if (dx, dy, dz) != (0, 0, 0)]


def as_f32(flag):
    return jnp.where(flag, 1.0, 0.0).astype(F32)


def axis_terms(at, width, low, high, place, count):
    inside = (place * width + at >= 0) & (place * width + at < count * width)
    cover = ((at == -1) | (at == 0)) & low | ((at == width - 1) | (at == width)) & high
    inner = ((at == -2) | (at == 1)) & low | ((at == width - 2) | (at == width + 1)) & high
    below = (at == 1) & low | (at == width + 1) & high
    above = (at == -2) & low | (at == width - 2) & high
    mask = as_f32(inside)
    return (1.0 + as_f32(cover)) * mask, as_f32(inner), 1.0 - 0.5 * as_f32(below), 1.0 - 0.5 * as_f32(above), mask


def kernel(
    counts, dims, near, res_ref, dir_ref, pow_ref, gram_ref, proj_ref,
    raw, main, pack, got, face, flat, cbuf, czbuf, sbuf, szbuf, image, zsum, zzsum, tab, ztab, half_tab, d_tab, g_tab, t_ref, red0, red1, spare,
    in_sem, out_sem, s_sem, r_sem, s0_sem, r0_sem, s1_sem, r1_sem,
):
    nx, ny, nz = counts
    cx, cy, cz = dims
    group = LANES // cx
    half = group // 2
    rows = 3 * cy
    place = [lax.axis_index(a) for a in AXES]
    gx, gy, gz = place
    low = [place[i] > 0 for i in range(3)]
    high = [place[i] < counts[i] - 1 for i in range(3)]
    total = 2 * STEPS + 1

    def exists(offset):
        ok = None
        for i, step in enumerate(offset):
            if step:
                test = low[i] if step < 0 else high[i]
                ok = test if ok is None else jnp.logical_and(ok, test)
        return ok

    def flip(offset):
        return tuple(-s for s in offset)

    def target(offset):
        return {AXES[i]: place[i] + s for i, s in enumerate(offset) if s}

    def ahead(axes):
        def make(k):
            out = {}
            for a in reversed(axes):
                k, step = divmod(k, counts[AXES.index(a)])
                if step:
                    out[a] = lax.rem(place[AXES.index(a)] + step, counts[AXES.index(a)])
            return out
        size = 1
        for a in axes:
            size *= counts[AXES.index(a)]
        return size, make

    loads = [
        pltpu.make_async_copy(ref, raw.at[c, 0, pl.ds(cx, cx), pl.ds(cy, cy)], in_sem.at[c])
        for c, ref in ((Z_CHAIN, res_ref), (P_CHAIN, dir_ref))
    ]
    for copy in loads:
        copy.start()

    barrier = pltpu.get_barrier_semaphore()
    expected = 0
    far_first = sorted(range(len(OFFSETS)), key=lambda i: -sum(abs(v) for v in OFFSETS[i]))
    for offset in [OFFSETS[i] for i in far_first]:
        @pl.when(exists(offset))
        def _():
            pl.semaphore_signal(barrier, 1, device_id=target(offset), device_id_type=MESH)
        expected = expected + exists(offset).astype(jnp.int32)
    if not near:
        for axes in (("gy", "gz"), ("gx",)):
            size, make = ahead(axes)
            for k in range(1, size):
                pl.semaphore_signal(barrier, 1, device_id=make(k), device_id_type=MESH)
            expected = expected + (size - 1)

    row = lax.broadcasted_iota(jnp.int32, (cy, LANES), 0)
    lane = lax.broadcasted_iota(jnp.int32, (cy, LANES), 1)
    top, bottom = row == 0, row == cy - 1
    runs = 3 * cx // RUN
    slot = (lane + half) // group % cx
    deep = (lane + half) % group - half
    is_hi = deep >= 0
    at_first, at_last = deep == 0, deep == -1
    is_first = [lane == group * g for g in range(runs)]
    is_last = [lane == (group * g - 1) % LANES for g in range(runs)]
    is_edge = [is_first[g] | is_last[g] for g in range(runs)]

    def x_terms(x):
        return axis_terms(jnp.int32(x), cx, low[0], high[0], gx, nx)

    below_1, above_6 = x_terms(1)[2], x_terms(cx - 2)[3]

    def turn(x):
        return group * ((x + cx) // RUN)

    TALL, SHORT = 3, 2
    AM0, M0, UPY, DOWNY = 0, 3, 6, 7
    ZD, ZAM, ZM, ZG, ZUX, ZDX = (RUN * k for k in range(6))

    def fill_tables():
        half_z = 1.0 - 0.5 * (as_f32((lane == 0) & low[2]) + as_f32((lane == LANES - 1) & high[2]))
        for g in range(runs):
            half_tab[g] = roll_lanes(half_z, group * g)
        half_tab[runs] = 1.0 - 0.5 * as_f32(at_first | at_last)
        wz, fz, _, _, mz = axis_terms(lane, cz, low[2], high[2], gz, nz)
        z_at = jnp.where(is_hi, deep + cz, deep)
        wzz, fzz, _, _, mzz = axis_terms(z_at, cz, low[2], high[2], gz, nz)
        along = [axis_terms(slot * RUN + (b - cx), cx, low[0], high[0], gx, nx) for b in range(RUN)]
        for high_rows in (TALL, SHORT):
            t = TALL - high_rows
            for k in range(high_rows):
                ds = pl.ds(k * cy, cy)
                if high_rows == TALL:
                    y = row + (k - 1) * cy
                elif k == 0:
                    y = jnp.where(row < cy // 2, row + cy, row - cy)
                else:
                    y = row
                wy, fy, up_y, down_y, my = axis_terms(y, cy, low[1], high[1], gy, ny)
                wyz, myz, gyz = wy * wz, my * mz, GAMMA + DELTA * (fy + fz)
                for n, x in enumerate((-3, 3, cx + 2)):
                    mask = myz * x_terms(x)[4]
                    tab[t, AM0 + n, ds] = mask * ALPHA
                    tab[t, M0 + n, ds] = mask
                tab[t, UPY, ds], tab[t, DOWNY, ds] = up_y, down_y
                for g in range(runs):
                    d_run, g_run = roll_lanes(wyz, group * g), roll_lanes(gyz, group * g)
                    for n in range(RUN * g, RUN * g + RUN):
                        cover, inner = x_terms(n - cx)[:2]
                        d_tab[t, n, ds] = d_run * cover
                        g_tab[t, n, ds] = g_run + DELTA * inner
                for b in range(RUN):
                    wx, fx, up_x, down_x, mx = along[b]
                    ztab[t, ZD + b, ds] = wx * wy * wzz
                    ztab[t, ZAM + b, ds] = mx * my * mzz * ALPHA
                    ztab[t, ZM + b, ds] = mx * my * mzz
                    ztab[t, ZG + b, ds] = GAMMA + DELTA * (fx + fy + fzz)
                    ztab[t, ZUX + b, ds] = up_x
                    ztab[t, ZDX + b, ds] = down_x

    def fill_zeros():
        fields = [(c, f) for c in (0, 1) for f in (0, 1)]
        for flag, xs, ys in (
            (low[0], pl.ds(0, cx), pl.ds(0, rows)), (high[0], pl.ds(2 * cx, cx), pl.ds(0, rows)),
            (low[1], pl.ds(0, 3 * cx), pl.ds(0, cy)), (high[1], pl.ds(0, 3 * cx), pl.ds(2 * cy, cy)),
        ):
            @pl.when(jnp.logical_not(flag))
            def _():
                for c, f in fields:
                    raw[c, f, xs, ys] = jnp.zeros((xs.size, ys.size, LANES), F32)
        for flag, ss, xs, ys in (
            (low[2], 0, pl.ds(0, 3), pl.ds(0, rows)), (high[2], 1, pl.ds(0, 3), pl.ds(0, rows)),
            (low[0], None, pl.ds(0, 1), pl.ds(0, rows)), (high[0], None, pl.ds(2, 1), pl.ds(0, rows)),
            (low[1], None, pl.ds(0, 3), pl.ds(0, cy)), (high[1], None, pl.ds(0, 3), pl.ds(2 * cy, cy)),
        ):
            @pl.when(jnp.logical_not(flag))
            def _():
                for c in (0, 1):
                    for s in (0, 1):
                        for side in ((0, 1) if ss is None else (ss,)):
                            got[c, s, side, xs, ys] = jnp.zeros((xs.size, ys.size, LANES), F32)

    def roll_rows(v, shift):
        return pltpu.roll(v, shift % v.shape[0], 0)

    def roll_lanes(v, shift):
        shift = shift % LANES
        return v if shift == 0 else pltpu.roll(v, shift, 1)

    def planes(reach):
        xs = list(range(-reach, cx + reach))
        return [xs[i:i + CHUNK] for i in range(0, len(xs), CHUNK)]

    def table(t, at, xs, n):
        ks = [at + (x + cx) // cx for x in xs]
        if len(set(ks)) == 1:
            return tab[t, ks[0], pl.ds(0, n)][None]
        return jnp.stack([tab[t, k, pl.ds(0, n)] for k in ks])

    def spread(v, tiles):
        return jnp.concatenate([v] * tiles, axis=0)

    def wide(mask, tiles):
        return jnp.concatenate([mask] * tiles, axis=0)

    def put(dst, xs, value, reach, tiles):
        for i, x in enumerate(xs):
            if reach > 0 and -reach < x < cx + reach - 1:
                dst[x + cx, pl.ds(0, tiles * cy)] = value[i]
            else:
                dst[x + cx, pl.ds(cy, cy)] = value[i, cy:2 * cy]

    flips = [0]

    def stream(src, z_src, reach, weighted, tiles):
        flips[0] ^= 1
        out, z_out = zsum.at[flips[0]], zzsum.at[flips[0]]
        t, n = TALL - tiles, tiles * cy
        ds = pl.ds(0, n)
        for x in range(-reach, cx + reach):
            g, b = divmod(x + cx, RUN)
            mid, extra = src[x + cx, ds], z_src[b, ds]
            if weighted:
                mid = mid * spread(half_tab[g], tiles)
            up = roll_lanes(jnp.where(wide(is_last[g], tiles), extra, mid), 1)
            down = roll_lanes(jnp.where(wide(is_first[g], tiles), extra, mid), -1)
            part = up + down
            if b == 0:
                part = part + roll_lanes(src[x + cx - 1, ds], group)
            if b == RUN - 1:
                part = part + roll_lanes(src[x + cx + 1, ds], -group)
            put(out, [x], part[None], reach, tiles)
        for b in range(RUN if reach > 0 else 0):
            mid = z_src[b, ds]
            inject = jnp.zeros((n, LANES), F32)
            for g in range(runs):
                x = g * RUN + b - cx
                if -reach <= x < cx + reach:
                    inject = jnp.where(wide(is_edge[g], tiles), src[x + cx, ds], inject)
            if weighted:
                mid = mid * spread(half_tab[runs], tiles)
            part = roll_lanes(jnp.where(wide(at_last, tiles), inject, mid), 1)
            part = part + roll_lanes(jnp.where(wide(at_first, tiles), inject, mid), -1)
            if b == 0:
                before = roll_lanes(z_src[RUN - 1, ds], group)
                part = part + (before * ztab[t, ZUX, ds] if weighted else before)
            if b == RUN - 1:
                after = roll_lanes(z_src[0, ds], -group)
                part = part + (after * ztab[t, ZDX + b, ds] if weighted else after)
            z_out[b, ds] = part
        return out, z_out

    def along_y(parts, weighted, tiles):
        t = TALL - tiles
        ahead_of = [pltpu.roll(v, 1, v.ndim - 2) for v in parts]
        behind = [pltpu.roll(v, cy - 1, v.ndim - 2) for v in parts]
        sums = []
        for k in range(tiles):
            left, right = ahead_of[k], behind[k]
            before = k - 1 if tiles == TALL else 1 - k
            after = k + 1 if tiles == TALL else 1 - k
            if before >= 0:
                left = jnp.where(top, ahead_of[before], left)
            if after < tiles:
                right = jnp.where(bottom, behind[after], right)
            if weighted and not (tiles == TALL and k == 0):
                left = left * tab[t, UPY, pl.ds(k * cy, cy)]
            if weighted and not (tiles == TALL and k == 2):
                right = right * tab[t, DOWNY, pl.ds(k * cy, cy)]
            sums.append(left + right)
        return jnp.concatenate(sums, axis=-2)

    def beside(src, sums, xs, weighted, tiles):
        lo = xs[0] + cx
        ds = pl.ds(0, tiles * cy)
        mid = src[pl.ds(lo, len(xs)), ds]
        parts = []
        for x in xs:
            b = (x + cx) % RUN
            part = sums[x + cx, ds]
            if b > 0:
                value = src[x + cx - 1, ds]
                if weighted and x == 1:
                    value = value * below_1
                if weighted and x == cx + 1:
                    value = value * 0.5
                part = part + value
            if b < RUN - 1:
                value = src[x + cx + 1, ds]
                if weighted and x == cx - 2:
                    value = value * above_6
                if weighted and x == -2:
                    value = value * 0.5
                part = part + value
            columns = [src[x + cx, pl.ds(k * cy, cy)] for k in range(tiles)]
            parts.append(part + along_y(columns, weighted, tiles))
        return mid, jnp.stack(parts)

    def z_beside(z_src, z_sums, b, weighted, tiles):
        t, ds = TALL - tiles, pl.ds(0, tiles * cy)
        around = z_sums[b, ds] + along_y([z_src[b, pl.ds(k * cy, cy)] for k in range(tiles)], weighted, tiles)
        if b > 0:
            value = z_src[b - 1, ds]
            around = around + (value * ztab[t, ZUX + b, ds] if weighted else value)
        if b < RUN - 1:
            value = z_src[b + 1, ds]
            around = around + (value * ztab[t, ZDX + b, ds] if weighted else value)
        return z_src[b, ds], around

    def shorten(v):
        outer = jnp.where(row < cy // 2, v[..., 2 * cy:, :], v[..., :cy, :])
        return jnp.concatenate([outer, v[..., cy:2 * cy, :]], axis=-2)

    def apply_a(c, f, reach, index, tiles):
        t, n = TALL - tiles, tiles * cy
        src, z_src = main.at[c, f], pack.at[c, f]
        sums, z_sums = stream(src, z_src, reach, False, tiles)
        for b in range(RUN if reach > 0 else 0):
            mid, around = z_beside(z_src, z_sums, b, False, tiles)
            czbuf[c, b, pl.ds(0, n)] = (6.0 * mid - around) * ztab[t, ZD + b, pl.ds(0, n)]
        for xs in planes(reach):
            mid, around = beside(src, sums, xs, False, tiles)
            value = 6.0 * mid - around
            for i, x in enumerate(xs):
                if 0 <= x < cx:
                    image[index, x] = value[i, cy:2 * cy]
            if reach > 0:
                ds = pl.ds(xs[0] + cx, len(xs))
                put(cbuf.at[c], xs, value * d_tab[t, ds, pl.ds(0, n)], reach, tiles)

    def scale_only(c, f, reach):
        for b in range(RUN):
            czbuf[c, b] = pack[c, f, b] * ztab[0, ZD + b]
        for xs in planes(reach):
            ds = pl.ds(xs[0] + cx, len(xs))
            put(cbuf.at[c], xs, main[c, f, ds] * d_tab[0, ds], reach, TALL)

    def apply_m(c, f, reach, tiles):
        t, n = TALL - tiles, tiles * cy
        rows = pl.ds(0, n)
        src, z_src = cbuf.at[c], czbuf.at[c]
        sums, z_sums = stream(src, z_src, reach + 1, True, tiles)
        for b in range(RUN):
            mid, around = z_beside(z_src, z_sums, b, True, tiles)
            szbuf[c, b, rows] = BETA * mid + around * ztab[t, ZAM + b, rows]
        for xs in planes(reach + 1):
            mid, around = beside(src, sums, xs, True, tiles)
            put(sbuf.at[c], xs, BETA * mid + around * table(t, AM0, xs, n), reach + 1, tiles)
        s_src, sz_src = sbuf.at[c], szbuf.at[c]
        sums, z_sums = stream(s_src, sz_src, reach, True, tiles)
        for b in range(RUN if reach > 0 else 0):
            _, around = z_beside(sz_src, z_sums, b, True, tiles)
            value = z_src[b, rows] * ztab[t, ZG + b, rows] + around * ztab[t, ZM + b, rows]
            pack[c, f, b, pl.ds(0, SHORT * cy)] = shorten(value) if tiles == TALL else value
        for xs in planes(reach):
            ds = pl.ds(xs[0] + cx, len(xs))
            _, around = beside(s_src, sums, xs, True, tiles)
            value = src[ds, rows] * g_tab[t, ds, rows]
            if reach > 0:
                value = value + around * table(t, M0, xs, n)
            else:
                value = value + around
            if tiles == TALL:
                value = shorten(value)
            put(main.at[c, f], xs, value, reach, SHORT)

    def parts_of(c, s, index):
        dx, dy, dz = OFFSETS[index]
        reach = REACH[s][c]
        if dz or dx == 0:
            return [(0, cx, cy)]
        if dy == 0:
            return [(0, reach, cy)]
        full = max(0, reach - cy // 2 - 1)
        return [p for p in ((0, full, cy), (full, reach - 1 - full, cy // 2)) if p[1] > 0]

    def copy_to(c, s, index, part):
        dx, dy, dz = OFFSETS[index]
        if dz == 0:
            skip, n, h = part
            first = cx + skip if dx <= 0 else 2 * cx - skip - n
            here = pl.ds(cy if dy <= 0 else 2 * cy - h, h)
            there = pl.ds(here.start - cy * dy, h)
            source = raw.at[c, s, pl.ds(first, n), here]
            sink = raw.at[c, s, pl.ds(first - cx * dx, n), there]
        else:
            source = face.at[c, s]
            sink = got.at[c, s, 0 if dz > 0 else 1, 1 - dx, pl.ds(cy - cy * dy, cy)]
        return pltpu.make_async_remote_copy(
            source, sink, s_sem.at[0], r_sem.at[c, s],
            device_id=target(OFFSETS[index]), device_id_type=MESH)

    per_block = cx // RUN

    def pack_face(c, s):
        value = jnp.zeros((cy, LANES), F32)
        for i in range(RUN):
            joined = main[c, 2 * s, cx + i, pl.ds(cy, cy)]
            for h in range(1, per_block):
                other = main[c, 2 * s, cx + h * RUN + i, pl.ds(cy, cy)]
                joined = jnp.where(slot == per_block + h, other, joined)
            moved = roll_lanes(joined, group * (per_block * i - per_block))
            value = jnp.where(slot // per_block == i, moved, value)
        face[c, s] = value

    def turn_own(c):
        for x in range(cx):
            main[c, 0, x + cx, pl.ds(cy, cy)] = roll_lanes(raw[c, 0, x + cx, pl.ds(cy, cy)], turn(x))

    def turn_back(c, f, out):
        for x in range(cx):
            out[x] = roll_lanes(main[c, f, x + cx, pl.ds(cy, cy)], -turn(x))

    def send(c, s):
        for index in far_first:
            @pl.when(exists(OFFSETS[index]))
            def _():
                for part in parts_of(c, s, index):
                    copy_to(c, s, index, part).start()

    around_it = [low[i].astype(jnp.int32) + high[i].astype(jnp.int32) for i in range(3)]
    choices = [{1: (0,), 2: (1,)}.get(n, (1, 2)) for n in counts]

    def tiles_of(c, s, ax, ay, az):
        sizes = {o: sum(n * h for _, n, h in parts_of(c, s, i)) for i, o in enumerate(OFFSETS)}
        in_rows = ax * sizes[1, 0, 0] + ay * sizes[0, 1, 0] + ax * ay * sizes[1, 1, 0]
        return (in_rows + az * (1 + ax) * (1 + ay) * cy) // 4

    def wait_bytes(sem, tiles):
        view = spare.at[pl.ds(0, tiles)]
        pltpu.make_async_copy(view, view, sem).wait()

    def wait_exchanges(sem, pairs):
        for ax in choices[0]:
            for ay in choices[1]:
                for az in choices[2]:
                    here = (around_it[0] == ax) & (around_it[1] == ay) & (around_it[2] == az)
                    tiles = sum(tiles_of(c, s, ax, ay, az) for c, s in pairs)
                    if tiles:
                        @pl.when(here)
                        def _():
                            wait_bytes(sem, tiles)

    def receive(c, s):
        wait_exchanges(r_sem.at[c, s], [(c, s)])
        f = 2 * s
        hi, at_block = wide(is_hi, TALL), [wide(slot // per_block == k, TALL) for k in range(3)]
        faces = [jnp.where(hi, got[c, s, 1, k], got[c, s, 0, k]) for k in range(3)]
        for b in range(RUN):
            value = jnp.zeros((TALL * cy, LANES), F32)
            for k in range(3):
                moved = roll_lanes(faces[k], group * per_block * (k - b))
                value = jnp.where(at_block[k], moved, value)
            pack[c, f, b] = value
        for x in range(-REACH[s][c], cx + REACH[s][c]):
            if 0 <= x < cx:
                for y in (0, 2 * cy):
                    main[c, f, x + cx, pl.ds(y, cy)] = roll_lanes(raw[c, s, x + cx, pl.ds(y, cy)], turn(x))
            else:
                main[c, f, x + cx] = roll_lanes(raw[c, s, x + cx], turn(x))

    def own(c, f):
        return main[c, f, pl.ds(cx, cx), pl.ds(cy, cy)].reshape(cx * cy, LANES)

    def emit(c, f, slot_out):
        turn_back(c, f, pow_ref.at[c, slot_out])

    place_of = {a: (P_CHAIN, a) for a in range(STEPS + 1)}
    place_of.update({STEPS + 1 + k: (Z_CHAIN, k + 1) for k in range(STEPS)})
    ready = []

    def account(a):
        ready.append(a)
        picture = image[a].reshape(cx * cy, LANES)
        for b in ready:
            part = jnp.sum(own(*place_of[b]) * picture, axis=0, keepdims=True)
            t_ref[pl.ds(a * total + b, 1), :] = part
            if a != b:
                t_ref[pl.ds(b * total + a, 1), :] = part
        t_ref[pl.ds(total * total + a, 1), :] = jnp.sum(
            own(*place_of[a]) * own(Z_CHAIN, 0), axis=0, keepdims=True)

    for copy in loads:
        copy.wait()
    for c in (Z_CHAIN, P_CHAIN):
        value = jnp.zeros((cy, LANES), F32)
        for x in range(cx):
            at = per_block * (x % RUN) + x // RUN
            value = jnp.where(slot == at, roll_lanes(raw[c, 0, x + cx, pl.ds(cy, cy)], group * at), value)
        face[c, 0] = value
    pl.semaphore_wait(barrier, expected)
    for c in (Z_CHAIN, P_CHAIN):
        send(c, 0)
    for c in (Z_CHAIN, P_CHAIN):
        turn_own(c)
    fill_zeros()
    fill_tables()
    t_ref[...] = jnp.zeros_like(t_ref)

    def finish_first(c):
        turn_back(c, 2, raw.at[c, 1, pl.ds(cx, cx), pl.ds(cy, cy)])
        pack_face(c, 1)
        send(c, 1)

    first_z = STEPS + 1
    receive(Z_CHAIN, 0)
    scale_only(Z_CHAIN, 0, 5)
    apply_m(Z_CHAIN, 1, 3, TALL)
    apply_a(Z_CHAIN, 1, 2, first_z, SHORT)
    apply_m(Z_CHAIN, 2, 0, SHORT)
    finish_first(Z_CHAIN)

    receive(P_CHAIN, 0)
    apply_a(P_CHAIN, 0, 5, 0, TALL)
    apply_m(P_CHAIN, 1, 3, TALL)
    apply_a(P_CHAIN, 1, 2, 1, SHORT)
    apply_m(P_CHAIN, 2, 0, SHORT)
    finish_first(P_CHAIN)
    for c in (Z_CHAIN, P_CHAIN):
        emit(c, 1, 0)
        emit(c, 2, 1)
    for a in (0, 1, first_z):
        account(a)

    receive(Z_CHAIN, 1)
    apply_a(Z_CHAIN, 2, 6, first_z + 1, TALL)
    apply_m(Z_CHAIN, 3, 4, TALL)
    apply_a(Z_CHAIN, 3, 3, first_z + 2, SHORT)
    apply_m(Z_CHAIN, 4, 1, SHORT)
    apply_a(Z_CHAIN, 4, 0, first_z + 3, SHORT)
    for k in (1, 2, 3):
        account(first_z + k)
    for k in (3, 4):
        emit(Z_CHAIN, k, k - 1)

    receive(P_CHAIN, 1)
    apply_a(P_CHAIN, 2, 6, 2, TALL)
    account(2)
    apply_m(P_CHAIN, 3, 4, TALL)
    emit(P_CHAIN, 3, 2)
    apply_a(P_CHAIN, 3, 3, 3, SHORT)
    account(3)
    apply_m(P_CHAIN, 4, 1, SHORT)
    emit(P_CHAIN, 4, 3)
    apply_a(P_CHAIN, 4, 0, 4, SHORT)
    account(4)

    value = lax.dot_general(
        jnp.ones((8, LANES), F32), t_ref[...], (((1,), (1,)), ((), ())),
        precision=HIGHEST, preferred_element_type=F32)[0:1]

    def far_order(size, axes):
        def hops(k):
            far = 0
            for a in reversed(axes):
                n = counts[AXES.index(a)]
                k, step = divmod(k, n)
                far += min(step, n - step)
            return -far
        return sorted(range(1, size), key=hops)

    def gather(value, axes, buffer, send_sem, recv_sem, meanwhile=lambda: None):
        size, make = ahead(axes)
        buffer[0] = value

        def copy(k):
            return pltpu.make_async_remote_copy(
                buffer.at[0], buffer.at[k], send_sem.at[0], recv_sem.at[0],
                device_id=make(k), device_id_type=MESH)

        for k in far_order(size, axes):
            copy(k).start()
        meanwhile()
        rest = buffer.at[pl.ds(1, size - 1)]
        pltpu.make_async_copy(rest, rest, send_sem.at[0]).wait()
        pltpu.make_async_copy(rest, rest, recv_sem.at[0]).wait()
        result = jnp.zeros_like(value)
        for k in range(size):
            rest, at = k, 0
            scale = 1
            for a in reversed(axes):
                n = counts[AXES.index(a)]
                rest, want = divmod(rest, n)
                at = at + scale * lax.rem(place[AXES.index(a)] + n - want, n)
                scale *= n
            result = result + buffer[at]
        return result

    def finish():
        wait_exchanges(s_sem.at[0], [(c, s) for c in (0, 1) for s in (0, 1)])

    if near:
        value = gather(value, AXES, red0, s0_sem, r0_sem, finish)
    else:
        value = gather(value, ("gy", "gz"), red0, s0_sem, r0_sem, finish)
        value = gather(value, ("gx",), red1, s1_sem, r1_sem)
    value = value * (1.0 / (nx * cx * ny * cy * nz * cz))
    for a in range(total):
        gram_ref[a:a + 1, :] = value[0:1, a * total:(a + 1) * total]
    proj_ref[...] = value[0:1, total * total:total * total + total]


def store(pow_ref, gram_ref, proj_ref, pow_out, gram_out, proj_out, sem):
    pairs = ((pow_ref, pow_out), (gram_ref, gram_out), (proj_ref, proj_out))
    copies = [pltpu.make_async_copy(a, b, sem.at[i]) for i, (a, b) in enumerate(pairs)]
    for copy in copies:
        copy.start()
    for copy in copies:
        copy.wait()


def solution(mesh):
    counts = tuple(mesh.shape[a] for a in AXES)
    near = max(counts) <= 4
    devices = counts[0] * counts[1] * counts[2]
    plane = devices if near else counts[1] * counts[2]

    def local(residual, direction):
        dims = residual.shape
        cx, cy, cz = dims
        assert cz == LANES and LANES % cx == 0 and cy % 8 == 0
        assert min(cx, cy, LANES // cx // 2) > max(max(r) for r in REACH)
        total = 2 * STEPS + 1
        fields = STEPS + 1
        dma = pltpu.SemaphoreType.DMA
        vm = pl.BlockSpec(memory_space=pltpu.VMEM)
        hbm = pl.BlockSpec(memory_space=pltpu.HBM)
        ext = (3 * cx, 3 * cy, LANES)
        zext = (RUN, 3 * cy, LANES)
        powers, gram, proj = pl.pallas_call(
            functools.partial(kernel, counts, dims, near),
            out_shape=(
                jax.ShapeDtypeStruct((2, STEPS) + dims, F32),
                jax.ShapeDtypeStruct((total, total), F32),
                jax.ShapeDtypeStruct((1, total), F32),
            ),
            in_specs=[hbm, hbm],
            out_specs=(vm, vm, vm),
            scratch_shapes=[
                pltpu.VMEM((2, 2) + ext, F32),
                pltpu.VMEM((2, fields) + ext, F32),
                pltpu.VMEM((2, fields) + zext, F32),
                pltpu.VMEM((2, 2, 2, 3, 3 * cy, LANES), F32),
                pltpu.VMEM((2, 2, cy, LANES), F32),
                pltpu.VMEM((2, STEPS) + dims, F32),
                pltpu.VMEM((2,) + ext, F32),
                pltpu.VMEM((2,) + zext, F32),
                pltpu.VMEM((2,) + ext, F32),
                pltpu.VMEM((2,) + zext, F32),
                pltpu.VMEM((total,) + dims, F32),
                pltpu.VMEM((2,) + ext, F32),
                pltpu.VMEM((2,) + zext, F32),
                pltpu.VMEM((2, 8, 3 * cy, LANES), F32),
                pltpu.VMEM((2, 6 * RUN, 3 * cy, LANES), F32),
                pltpu.VMEM((3 * cx // RUN + 1, cy, LANES), F32),
                pltpu.VMEM((2,) + ext, F32),
                pltpu.VMEM((2,) + ext, F32),
                pltpu.VMEM((LANES, LANES), F32),
                pltpu.VMEM((plane, 1, LANES), F32),
                pltpu.VMEM((counts[0], 1, LANES), F32),
                pltpu.VMEM((4 * 9 * cx * (cy // 4), 4, LANES), F32),
                dma((2,)), dma((1,)),
                dma((1,)), dma((2, 2)),
                dma((1,)), dma((1,)),
                dma((1,)), dma((1,)),
            ],
            compiler_params=pltpu.CompilerParams(collective_id=0, has_side_effects=True, vmem_limit_bytes=24 << 20),
            name="powers_basis",
        )(*[pltpu.with_memory_space_constraint(v, pltpu.HBM) for v in (residual, direction)])
        powers, gram, proj = pl.pallas_call(
            store,
            out_shape=(
                jax.ShapeDtypeStruct((2, STEPS) + dims, F32),
                jax.ShapeDtypeStruct((total, total), F32),
                jax.ShapeDtypeStruct((1, total), F32),
            ),
            in_specs=[vm, vm, vm],
            out_specs=(hbm, hbm, hbm),
            scratch_shapes=[dma((3,))],
            compiler_params=pltpu.CompilerParams(vmem_limit_bytes=1 << 20),
            name="store",
        )(powers, gram, proj)
        return powers, gram, proj.reshape(total)

    placed = (P("gx", "gy", "gz"), P("gx", "gy", "gz"))
    return jax.shard_map(
        local,
        mesh=mesh,
        in_specs=placed,
        out_specs=(P(None, None, "gx", "gy", "gz"), P(), P()),
        check_vma=False,
    )
```

time: 23.4 us -> 22 us (0.940)
  Pallas kernels: 22.5 us -> 21.2 us
    pallas_call x1, Pallas kernels: 21.8 us -> 20.5 us  [local(): pl.pallas_call(functools.partial(kernel, counts, dims, near), out_shape=(...]
where the time goes in v4:
time: 22 us; the launch traced here: 21.9 us
  Pallas kernels  21.2 us (96%)
  between operations  0.64 us (3%)
    pallas_call x1, Pallas kernels, local(): pl.pallas_call(functools.partial(kernel, counts, dims, near), out_shape=(...  20.5 us
    pallas_call x1, Pallas kernels, local(): pl.pallas_call(store, out_shape=(jax.ShapeDtypeStruct((2, STEPS) + dims,...  0.74 us

profile of v4, /device:TPU:0, one launch (start us, length us, event | category | flops | bytes accessed | tf_op | source)
XLA Modules:
  0.0 21.9 jit_solution(14893453244654290840)
XLA Ops:
  0.6 20.5 %powers_basis.1 = (f32[2,4,8,8,128]{4,3,2,1,0:T(8,128)S(1)}, f32[9,9]{1,0:T(8,128)S(1)}, f32[1,9]{1,0:T(1,128)S(1)}) custom-call(f32[8,8,128]{2,1,0:T(8,128)} %res_ref.1, f32[8,8,128]{2,1,0:T(8,128)} %dir_ref.1), custom_call_target="tpu_custom_call" | custom-call | tf_op jit(solution)/shard_map/powers_basis/pallas_call | solution.py:637
  21.1 0.7 %store.1 = (f32[2,4,8,8,128]{4,3,2,1,0:T(8,128)}, f32[9,9]{1,0:T(8,128)}, f32[1,9]{1,0:T(1,128)}) custom-call(f32[2,4,8,8,128]{4,3,2,1,0:T(8,128)S(1)} %get-tuple-element.9.pow_ref, f32[9,9]{1,0:T(8,128)S(1)} %get-tuple-element.10.gram_ref, f32[1,9]{1,0:T(1,128)S(1)} %get-tuple-element.11.proj_ref), custom_call_target="tpu_custom_call" | custom-call | tf_op jit(solution)/shard_map/store/pallas_call | solution.py:677

commit v5 on v4

--- a/solution.py
+++ b/solution.py
@@ -15,7 +15,7 @@
 AXES = ("gx", "gy", "gz")
 GAMMA, BETA, ALPHA, DELTA = 13.0 / 81.0, 5.0 / 243.0, 1.0 / 729.0, 1.0 / 1458.0
 P_CHAIN, Z_CHAIN = 0, 1
-REACH = ((6, 5), (7, 7))
+REACH = ((7, 6), (6, 6))
 CHUNK = 4
 RUN = 4
 OFFSETS = [(dx, dy, dz) for dx in (-1, 0, 1) for dy in (-1, 0, 1) for dz in (-1, 0, 1) if (dx, dy, dz) != (0, 0, 0)]
@@ -331,16 +331,8 @@
             for i, x in enumerate(xs):
                 if 0 <= x < cx:
                     image[index, x] = value[i, cy:2 * cy]
-            if reach > 0:
-                ds = pl.ds(xs[0] + cx, len(xs))
-                put(cbuf.at[c], xs, value * d_tab[t, ds, pl.ds(0, n)], reach, tiles)
-
-    def scale_only(c, f, reach):
-        for b in range(RUN):
-            czbuf[c, b] = pack[c, f, b] * ztab[0, ZD + b]
-        for xs in planes(reach):
             ds = pl.ds(xs[0] + cx, len(xs))
-            put(cbuf.at[c], xs, main[c, f, ds] * d_tab[0, ds], reach, TALL)
+            put(cbuf.at[c], xs, value * d_tab[t, ds, pl.ds(0, n)], reach, tiles)
 
     def apply_m(c, f, reach, tiles):
         t, n = TALL - tiles, tiles * cy
@@ -374,7 +366,9 @@
     def parts_of(c, s, index):
         dx, dy, dz = OFFSETS[index]
         reach = REACH[s][c]
-        if dz or dx == 0:
+        if dz:
+            return [(0, 1, cy // 2 if dx and dy and reach - 2 <= cy // 2 else cy)]
+        if dx == 0:
             return [(0, cx, cy)]
         if dy == 0:
             return [(0, reach, cy)]
@@ -391,20 +385,22 @@
             source = raw.at[c, s, pl.ds(first, n), here]
             sink = raw.at[c, s, pl.ds(first - cx * dx, n), there]
         else:
-            source = face.at[c, s]
-            sink = got.at[c, s, 0 if dz > 0 else 1, 1 - dx, pl.ds(cy - cy * dy, cy)]
+            skip, n, h = part
+            here = pl.ds(0 if dy <= 0 else cy - h, h)
+            source = face.at[c, s, here]
+            sink = got.at[c, s, 0 if dz > 0 else 1, 1 - dx, pl.ds(here.start + cy - cy * dy, h)]
         return pltpu.make_async_remote_copy(
             source, sink, s_sem.at[0], r_sem.at[c, s],
             device_id=target(OFFSETS[index]), device_id_type=MESH)
 
     per_block = cx // RUN
 
-    def pack_face(c, s):
+    def pack_face(c, s, source):
         value = jnp.zeros((cy, LANES), F32)
         for i in range(RUN):
-            joined = main[c, 2 * s, cx + i, pl.ds(cy, cy)]
+            joined = source(i)
             for h in range(1, per_block):
-                other = main[c, 2 * s, cx + h * RUN + i, pl.ds(cy, cy)]
+                other = source(h * RUN + i)
                 joined = jnp.where(slot == per_block + h, other, joined)
             moved = roll_lanes(joined, group * (per_block * i - per_block))
             value = jnp.where(slot // per_block == i, moved, value)
@@ -414,9 +410,9 @@
         for x in range(cx):
             main[c, 0, x + cx, pl.ds(cy, cy)] = roll_lanes(raw[c, 0, x + cx, pl.ds(cy, cy)], turn(x))
 
-    def turn_back(c, f, out):
+    def turn_back(source, out):
         for x in range(cx):
-            out[x] = roll_lanes(main[c, f, x + cx, pl.ds(cy, cy)], -turn(x))
+            out[x] = roll_lanes(source(x), -turn(x))
 
     def send(c, s):
         for index in far_first:
@@ -431,7 +427,8 @@
     def tiles_of(c, s, ax, ay, az):
         sizes = {o: sum(n * h for _, n, h in parts_of(c, s, i)) for i, o in enumerate(OFFSETS)}
         in_rows = ax * sizes[1, 0, 0] + ay * sizes[0, 1, 0] + ax * ay * sizes[1, 1, 0]
-        return (in_rows + az * (1 + ax) * (1 + ay) * cy) // 4
+        in_rows += az * (sizes[0, 0, 1] + ax * sizes[1, 0, 1] + ay * sizes[0, 1, 1] + ax * ay * sizes[1, 1, 1])
+        return in_rows // 4
 
     def wait_bytes(sem, tiles):
         view = spare.at[pl.ds(0, tiles)]
@@ -450,7 +447,8 @@
 
     def receive(c, s):
         wait_exchanges(r_sem.at[c, s], [(c, s)])
-        f = 2 * s
+        scaled = s == 1 or c == Z_CHAIN
+        into, z_into = (cbuf.at[c], czbuf.at[c]) if scaled else (main.at[c, 0], pack.at[c, 0])
         hi, at_block = wide(is_hi, TALL), [wide(slot // per_block == k, TALL) for k in range(3)]
         faces = [jnp.where(hi, got[c, s, 1, k], got[c, s, 0, k]) for k in range(3)]
         for b in range(RUN):
@@ -458,19 +456,28 @@
             for k in range(3):
                 moved = roll_lanes(faces[k], group * per_block * (k - b))
                 value = jnp.where(at_block[k], moved, value)
-            pack[c, f, b] = value
-        for x in range(-REACH[s][c], cx + REACH[s][c]):
+            z_into[b] = value * ztab[0, ZD + b] if scaled else value
+        reach = REACH[s][c]
+        for x in range(-reach, cx + reach):
             if 0 <= x < cx:
-                for y in (0, 2 * cy):
-                    main[c, f, x + cx, pl.ds(y, cy)] = roll_lanes(raw[c, s, x + cx, pl.ds(y, cy)], turn(x))
+                ys = [0, 2 * cy]
+            elif x in (-reach, cx + reach - 1):
+                ys = [cy]
             else:
-                main[c, f, x + cx] = roll_lanes(raw[c, s, x + cx], turn(x))
+                ys = [0, cy, 2 * cy]
+            for y in ys:
+                ds = pl.ds(y, cy)
+                value = roll_lanes(raw[c, s, x + cx, ds], turn(x))
+                into[x + cx, ds] = value * d_tab[0, x + cx, ds] if scaled else value
+            if scaled and s == 0 and 0 <= x < cx:
+                ds = pl.ds(cy, cy)
+                into[x + cx, ds] = main[c, 0, x + cx, ds] * d_tab[0, x + cx, ds]
 
     def own(c, f):
         return main[c, f, pl.ds(cx, cx), pl.ds(cy, cy)].reshape(cx * cy, LANES)
 
     def emit(c, f, slot_out):
-        turn_back(c, f, pow_ref.at[c, slot_out])
+        turn_back(lambda x: main[c, f, x + cx, pl.ds(cy, cy)], pow_ref.at[c, slot_out])
 
     place_of = {a: (P_CHAIN, a) for a in range(STEPS + 1)}
     place_of.update({STEPS + 1 + k: (Z_CHAIN, k + 1) for k in range(STEPS)})
@@ -504,45 +511,43 @@
     fill_tables()
     t_ref[...] = jnp.zeros_like(t_ref)
 
-    def finish_first(c):
-        turn_back(c, 2, raw.at[c, 1, pl.ds(cx, cx), pl.ds(cy, cy)])
-        pack_face(c, 1)
+    def finish_first(c, index):
+        turn_back(lambda x: image[index, x], raw.at[c, 1, pl.ds(cx, cx), pl.ds(cy, cy)])
+        pack_face(c, 1, lambda x: image[index, x])
         send(c, 1)
 
     first_z = STEPS + 1
     receive(Z_CHAIN, 0)
-    scale_only(Z_CHAIN, 0, 5)
-    apply_m(Z_CHAIN, 1, 3, TALL)
-    apply_a(Z_CHAIN, 1, 2, first_z, SHORT)
-    apply_m(Z_CHAIN, 2, 0, SHORT)
-    finish_first(Z_CHAIN)
+    apply_m(Z_CHAIN, 1, 4, TALL)
+    apply_a(Z_CHAIN, 1, 3, first_z, SHORT)
+    apply_m(Z_CHAIN, 2, 1, SHORT)
+    apply_a(Z_CHAIN, 2, 0, first_z + 1, SHORT)
+    finish_first(Z_CHAIN, first_z + 1)
 
     receive(P_CHAIN, 0)
-    apply_a(P_CHAIN, 0, 5, 0, TALL)
-    apply_m(P_CHAIN, 1, 3, TALL)
-    apply_a(P_CHAIN, 1, 2, 1, SHORT)
-    apply_m(P_CHAIN, 2, 0, SHORT)
-    finish_first(P_CHAIN)
+    apply_a(P_CHAIN, 0, 6, 0, TALL)
+    apply_m(P_CHAIN, 1, 4, TALL)
+    apply_a(P_CHAIN, 1, 3, 1, SHORT)
+    apply_m(P_CHAIN, 2, 1, SHORT)
+    apply_a(P_CHAIN, 2, 0, 2, SHORT)
+    finish_first(P_CHAIN, 2)
     for c in (Z_CHAIN, P_CHAIN):
         emit(c, 1, 0)
         emit(c, 2, 1)
-    for a in (0, 1, first_z):
+    for a in (0, 1, 2, first_z, first_z + 1):
         account(a)
 
     receive(Z_CHAIN, 1)
-    apply_a(Z_CHAIN, 2, 6, first_z + 1, TALL)
     apply_m(Z_CHAIN, 3, 4, TALL)
     apply_a(Z_CHAIN, 3, 3, first_z + 2, SHORT)
     apply_m(Z_CHAIN, 4, 1, SHORT)
     apply_a(Z_CHAIN, 4, 0, first_z + 3, SHORT)
-    for k in (1, 2, 3):
+    for k in (2, 3):
         account(first_z + k)
     for k in (3, 4):
         emit(Z_CHAIN, k, k - 1)
 
     receive(P_CHAIN, 1)
-    apply_a(P_CHAIN, 2, 6, 2, TALL)
-    account(2)
     apply_m(P_CHAIN, 3, 4, TALL)
     emit(P_CHAIN, 3, 2)
     apply_a(P_CHAIN, 3, 3, 3, SHORT)

time: 22 us -> 21.9 us (level)
  no operation moved by 1% of the time
where the time goes in v5:
time: 21.9 us; the launch traced here: 21.7 us
  Pallas kernels  21.1 us (96%)
  between operations  0.64 us (3%)
    pallas_call x1, Pallas kernels, local(): pl.pallas_call(functools.partial(kernel, counts, dims, near), out_shape=(...  20.3 us
    pallas_call x1, Pallas kernels, local(): pl.pallas_call(store, out_shape=(jax.ShapeDtypeStruct((2, STEPS) + dims,...  0.74 us

profile of v5, /device:TPU:0, one launch (start us, length us, event | category | flops | bytes accessed | tf_op | source)
XLA Modules:
  0.0 21.7 jit_solution(13464018149663828641)
XLA Ops:
  0.6 20.3 %powers_basis.1 = (f32[2,4,8,8,128]{4,3,2,1,0:T(8,128)S(1)}, f32[9,9]{1,0:T(8,128)S(1)}, f32[1,9]{1,0:T(1,128)S(1)}) custom-call(f32[8,8,128]{2,1,0:T(8,128)} %res_ref.1, f32[8,8,128]{2,1,0:T(8,128)} %dir_ref.1), custom_call_target="tpu_custom_call" | custom-call | tf_op jit(solution)/shard_map/powers_basis/pallas_call | solution.py:642
  21.0 0.7 %store.1 = (f32[2,4,8,8,128]{4,3,2,1,0:T(8,128)}, f32[9,9]{1,0:T(8,128)}, f32[1,9]{1,0:T(1,128)}) custom-call(f32[2,4,8,8,128]{4,3,2,1,0:T(8,128)S(1)} %get-tuple-element.9.pow_ref, f32[9,9]{1,0:T(8,128)S(1)} %get-tuple-element.10.gram_ref, f32[1,9]{1,0:T(1,128)S(1)} %get-tuple-element.11.proj_ref), custom_call_target="tpu_custom_call" | custom-call | tf_op jit(solution)/shard_map/store/pallas_call | solution.py:682

commit v6 on v5

--- a/solution.py
+++ b/solution.py
@@ -15,7 +15,7 @@
 AXES = ("gx", "gy", "gz")
 GAMMA, BETA, ALPHA, DELTA = 13.0 / 81.0, 5.0 / 243.0, 1.0 / 729.0, 1.0 / 1458.0
 P_CHAIN, Z_CHAIN = 0, 1
-REACH = ((7, 6), (6, 6))
+REACH = ((7, 5), (6, 7))
 CHUNK = 4
 RUN = 4
 OFFSETS = [(dx, dy, dz) for dx in (-1, 0, 1) for dy in (-1, 0, 1) for dz in (-1, 0, 1) if (dx, dy, dz) != (0, 0, 0)]
@@ -447,8 +447,8 @@
 
     def receive(c, s):
         wait_exchanges(r_sem.at[c, s], [(c, s)])
-        scaled = s == 1 or c == Z_CHAIN
-        into, z_into = (cbuf.at[c], czbuf.at[c]) if scaled else (main.at[c, 0], pack.at[c, 0])
+        scaled = (s == 1) == (c == P_CHAIN)
+        into, z_into = (cbuf.at[c], czbuf.at[c]) if scaled else (main.at[c, 2 * s], pack.at[c, 2 * s])
         hi, at_block = wide(is_hi, TALL), [wide(slot // per_block == k, TALL) for k in range(3)]
         faces = [jnp.where(hi, got[c, s, 1, k], got[c, s, 0, k]) for k in range(3)]
         for b in range(RUN):
@@ -511,18 +511,17 @@
     fill_tables()
     t_ref[...] = jnp.zeros_like(t_ref)
 
-    def finish_first(c, index):
-        turn_back(lambda x: image[index, x], raw.at[c, 1, pl.ds(cx, cx), pl.ds(cy, cy)])
-        pack_face(c, 1, lambda x: image[index, x])
+    def finish_first(c, source):
+        turn_back(source, raw.at[c, 1, pl.ds(cx, cx), pl.ds(cy, cy)])
+        pack_face(c, 1, source)
         send(c, 1)
 
     first_z = STEPS + 1
     receive(Z_CHAIN, 0)
-    apply_m(Z_CHAIN, 1, 4, TALL)
-    apply_a(Z_CHAIN, 1, 3, first_z, SHORT)
-    apply_m(Z_CHAIN, 2, 1, SHORT)
-    apply_a(Z_CHAIN, 2, 0, first_z + 1, SHORT)
-    finish_first(Z_CHAIN, first_z + 1)
+    apply_m(Z_CHAIN, 1, 3, TALL)
+    apply_a(Z_CHAIN, 1, 2, first_z, SHORT)
+    apply_m(Z_CHAIN, 2, 0, SHORT)
+    finish_first(Z_CHAIN, lambda x: main[Z_CHAIN, 2, x + cx, pl.ds(cy, cy)])
 
     receive(P_CHAIN, 0)
     apply_a(P_CHAIN, 0, 6, 0, TALL)
@@ -530,19 +529,20 @@
     apply_a(P_CHAIN, 1, 3, 1, SHORT)
     apply_m(P_CHAIN, 2, 1, SHORT)
     apply_a(P_CHAIN, 2, 0, 2, SHORT)
-    finish_first(P_CHAIN, 2)
+    finish_first(P_CHAIN, lambda x: image[2, x])
     for c in (Z_CHAIN, P_CHAIN):
         emit(c, 1, 0)
         emit(c, 2, 1)
-    for a in (0, 1, 2, first_z, first_z + 1):
+    for a in (0, 1, 2, first_z):
         account(a)
 
     receive(Z_CHAIN, 1)
+    apply_a(Z_CHAIN, 2, 6, first_z + 1, TALL)
     apply_m(Z_CHAIN, 3, 4, TALL)
     apply_a(Z_CHAIN, 3, 3, first_z + 2, SHORT)
     apply_m(Z_CHAIN, 4, 1, SHORT)
     apply_a(Z_CHAIN, 4, 0, first_z + 3, SHORT)
-    for k in (2, 3):
+    for k in (1, 2, 3):
         account(first_z + k)
     for k in (3, 4):
         emit(Z_CHAIN, k, k - 1)

time: 21.9 us -> 21.6 us (0.986)
  Pallas kernels: 21.1 us -> 20.7 us
    pallas_call x1, Pallas kernels: 20.3 us -> 20 us  [local(): pl.pallas_call(functools.partial(kernel, counts, dims, near), out_shape=(...]
where the time goes in v6:
time: 21.6 us; the launch traced here: 21.4 us
  Pallas kernels  20.7 us (96%)
  between operations  0.64 us (3%)
    pallas_call x1, Pallas kernels, local(): pl.pallas_call(functools.partial(kernel, counts, dims, near), out_shape=(...  20 us
    pallas_call x1, Pallas kernels, local(): pl.pallas_call(store, out_shape=(jax.ShapeDtypeStruct((2, STEPS) + dims,...  0.74 us

profile of v6, /device:TPU:0, one launch (start us, length us, event | category | flops | bytes accessed | tf_op | source)
XLA Modules:
  0.0 21.4 jit_solution(11931293269437410832)
XLA Ops:
  0.6 20.0 %powers_basis.1 = (f32[2,4,8,8,128]{4,3,2,1,0:T(8,128)S(1)}, f32[9,9]{1,0:T(8,128)S(1)}, f32[1,9]{1,0:T(1,128)S(1)}) custom-call(f32[8,8,128]{2,1,0:T(8,128)} %res_ref.1, f32[8,8,128]{2,1,0:T(8,128)} %dir_ref.1), custom_call_target="tpu_custom_call" | custom-call | tf_op jit(solution)/shard_map/powers_basis/pallas_call | solution.py:642
  20.6 0.7 %store.1 = (f32[2,4,8,8,128]{4,3,2,1,0:T(8,128)}, f32[9,9]{1,0:T(8,128)}, f32[1,9]{1,0:T(1,128)}) custom-call(f32[2,4,8,8,128]{4,3,2,1,0:T(8,128)S(1)} %get-tuple-element.9.pow_ref, f32[9,9]{1,0:T(8,128)S(1)} %get-tuple-element.10.gram_ref, f32[1,9]{1,0:T(1,128)S(1)} %get-tuple-element.11.proj_ref), custom_call_target="tpu_custom_call" | custom-call | tf_op jit(solution)/shard_map/store/pallas_call | solution.py:682

commit v7 on v6

--- a/solution.py
+++ b/solution.py
@@ -573,11 +573,14 @@
 
     def gather(value, axes, buffer, send_sem, recv_sem, meanwhile=lambda: None):
         size, make = ahead(axes)
-        buffer[0] = value
+        mine = 0
+        for a in axes:
+            mine = mine * counts[AXES.index(a)] + place[AXES.index(a)]
+        buffer[mine] = value
 
         def copy(k):
             return pltpu.make_async_remote_copy(
-                buffer.at[0], buffer.at[k], send_sem.at[0], recv_sem.at[0],
+                buffer.at[mine], buffer.at[mine], send_sem.at[0], recv_sem.at[0],
                 device_id=make(k), device_id_type=MESH)
 
         for k in far_order(size, axes):
@@ -586,16 +589,10 @@
         rest = buffer.at[pl.ds(1, size - 1)]
         pltpu.make_async_copy(rest, rest, send_sem.at[0]).wait()
         pltpu.make_async_copy(rest, rest, recv_sem.at[0]).wait()
-        result = jnp.zeros_like(value)
-        for k in range(size):
-            rest, at = k, 0
-            scale = 1
-            for a in reversed(axes):
-                n = counts[AXES.index(a)]
-                rest, want = divmod(rest, n)
-                at = at + scale * lax.rem(place[AXES.index(a)] + n - want, n)
-                scale *= n
-            result = result + buffer[at]
+        parts = [buffer[k] for k in range(size)]
+        while len(parts) > 1:
+            parts = [sum(parts[i:i + 2][1:], parts[i]) for i in range(0, len(parts), 2)]
+        result = parts[0]
         return result
 
     def finish():

time: 21.6 us -> 21.5 us (level)
  no operation moved by 1% of the time
where the time goes in v7:
time: 21.5 us; the launch traced here: 21.4 us
  Pallas kernels  20.7 us (96%)
  between operations  0.64 us (3%)
    pallas_call x1, Pallas kernels, local(): pl.pallas_call(functools.partial(kernel, counts, dims, near), out_shape=(...  20 us
    pallas_call x1, Pallas kernels, local(): pl.pallas_call(store, out_shape=(jax.ShapeDtypeStruct((2, STEPS) + dims,...  0.74 us

profile of v7, /device:TPU:0, one launch (start us, length us, event | category | flops | bytes accessed | tf_op | source)
XLA Modules:
  0.0 21.4 jit_solution(6600636552350318836)
XLA Ops:
  0.6 20.0 %powers_basis.1 = (f32[2,4,8,8,128]{4,3,2,1,0:T(8,128)S(1)}, f32[9,9]{1,0:T(8,128)S(1)}, f32[1,9]{1,0:T(1,128)S(1)}) custom-call(f32[8,8,128]{2,1,0:T(8,128)} %res_ref.1, f32[8,8,128]{2,1,0:T(8,128)} %dir_ref.1), custom_call_target="tpu_custom_call" | custom-call | tf_op jit(solution)/shard_map/powers_basis/pallas_call | solution.py:639
  20.6 0.7 %store.1 = (f32[2,4,8,8,128]{4,3,2,1,0:T(8,128)}, f32[9,9]{1,0:T(8,128)}, f32[1,9]{1,0:T(1,128)}) custom-call(f32[2,4,8,8,128]{4,3,2,1,0:T(8,128)S(1)} %get-tuple-element.9.pow_ref, f32[9,9]{1,0:T(8,128)S(1)} %get-tuple-element.10.gram_ref, f32[1,9]{1,0:T(1,128)S(1)} %get-tuple-element.11.proj_ref), custom_call_target="tpu_custom_call" | custom-call | tf_op jit(solution)/shard_map/store/pallas_call | solution.py:679
